TPU v7x, 16 devices: a whole 2x2x2 slice. The times are simulated.
16 devices in a mesh: tp: 2 (over z), dp: 8 (over y, x, core).
Axes of the slice: x: 2, y: 2, z: 2, core: 2. Of those that a mesh axis runs over, the one named last changes fastest.
Arguments:
- feats: bfloat16 [4096, 49, 1024], P('dp')
- ln_gamma: float32 [1024], replicated
- ln_beta: float32 [1024], replicated
- w_head: bfloat16 [1024, 22528], P(None, 'tp')
- b_head: float32 [22528], P('tp')
- labels: int32 [4096], P('dp')
Outputs:
- output 1: float32 [], replicated
- output 2: bfloat16 [4096, 49, 1024], P('dp')
- output 3: float32 [1024, 22528], P(None, 'tp')
- output 4: float32 [22528], P('tp')
- output 5: float32 [1024], replicated
- output 6: float32 [1024], replicated
All inputs are finite; a program needn't handle non-finite values.
Results may differ from a plain program's by a relative error of at most 0.001.
Values sent between devices are 32-bit elements.
A program may use at most 1 GiB of HBM per device.

v0:
```python
import jax
import jax.numpy as jnp
from jax import lax
from jax.sharding import PartitionSpec as P

VALID_CLASSES = 21841
LN_EPS = 1e-5
SMOOTH = 0.1


def norm_pool(feats, ln_gamma, ln_beta):
    x_val = feats.astype(jnp.float32)
    mean_x = jnp.mean(x_val, axis=-1, keepdims=True)
    centered = x_val - mean_x
    var_x = jnp.mean(centered * centered, axis=-1, keepdims=True)
    inv_std = lax.rsqrt(var_x + LN_EPS)
    x_hat = centered * inv_std
    x_hat_mean = jnp.mean(x_hat, axis=1)
    pooled16 = (x_hat_mean * ln_gamma + ln_beta).astype(jnp.bfloat16)
    return x_hat, inv_std, x_hat_mean, pooled16


def norm_backward(grad_pool, x_hat, inv_std, x_hat_mean, ln_gamma):
    token_count = x_hat.shape[1]
    grad_gamma = jnp.sum(grad_pool * x_hat_mean, axis=0)
    grad_beta = jnp.sum(grad_pool, axis=0)
    upstream = grad_pool * ln_gamma / token_count
    up_mean = jnp.mean(upstream, axis=-1)
    proj_term = jnp.mean(x_hat * upstream[:, None, :], axis=-1, keepdims=True)
    grad_x = inv_std * (upstream[:, None, :] - up_mean[:, None, None] - x_hat * proj_term)
    return grad_x.astype(jnp.bfloat16), grad_gamma, grad_beta


def solution(mesh):
    data_size = mesh.shape["dp"]

    def local_head(feats, ln_gamma, ln_beta, w_head, b_head, labels):
        shard_cols = w_head.shape[1]
        global_rows = feats.shape[0] * data_size
        x_hat, inv_std, x_hat_mean, pooled16 = norm_pool(feats, ln_gamma, ln_beta)
        col_ids = lax.axis_index("tp") * shard_cols + jnp.arange(shard_cols)
        valid_mask = col_ids < VALID_CLASSES
        logits = jnp.dot(pooled16, w_head, preferred_element_type=jnp.float32) + b_head
        logits = jnp.where(valid_mask, logits, -1e30)
        row_max = lax.pmax(jnp.max(logits, axis=-1), "tp")
        shifted = jnp.exp(logits - row_max[:, None])
        onehot = col_ids == labels[:, None]
        row_stats = jnp.stack([jnp.sum(shifted, axis=-1), jnp.sum(jnp.where(onehot, logits, 0.0), axis=-1), jnp.sum(jnp.where(valid_mask, logits, 0.0), axis=-1)])
        row_stats = lax.psum(row_stats, "tp")
        log_norm = row_max + jnp.log(row_stats[0])
        loss_rows = log_norm - (1.0 - SMOOTH) * row_stats[1] - (SMOOTH / VALID_CLASSES) * row_stats[2]
        soft_probs = shifted / row_stats[0][:, None]
        dlogit = (soft_probs - (1.0 - SMOOTH) * onehot - (SMOOTH / VALID_CLASSES) * valid_mask) / global_rows
        dlogit16 = dlogit.astype(jnp.bfloat16)
        grad_w = lax.psum(lax.dot_general(pooled16, dlogit16, (((0,), (0,)), ((), ())), preferred_element_type=jnp.float32), "dp")
        grad_b = lax.psum(jnp.sum(dlogit, axis=0), "dp")
        grad_pool = lax.dot_general(dlogit16, w_head, (((1,), (1,)), ((), ())), preferred_element_type=jnp.float32)
        grad_pool = lax.psum(grad_pool, "tp")
        grad_feats, grad_gamma, grad_beta = norm_backward(grad_pool, x_hat, inv_std, x_hat_mean, ln_gamma)
        loss_sum, grad_gamma, grad_beta = lax.psum((jnp.sum(loss_rows), grad_gamma, grad_beta), "dp")
        return loss_sum / global_rows, grad_feats, grad_w, grad_b, grad_gamma, grad_beta

    return jax.shard_map(local_head, mesh=mesh, in_specs=(P("dp", None, None), P(), P(), P(None, "tp"), P("tp"), P("dp")), out_specs=(P(), P("dp", None, None), P(None, "tp"), P("tp"), P(), P()), check_vma=False)
```

profile of v0, /device:TPU:0, one launch (start us, length us, event | category | flops | bytes accessed | tf_op | source)
XLA Modules:
  0.0 781.1 jit_solution(9062303119814713970)
XLA Ops:
  7.2 0.0 all-reduce.4.cloned.1.call-start
  7.3 0.7 broadcast_multiply_fusion.2
  8.0 16.5 %convert_reduce_fusion = f32[512,49]{0,1:T(8,128)S(1)} fusion(bf16[512,49,1024]{2,0,1:T(8,128)(2,1)} %param.6), kind=kLoop, calls=%fused_computation.1 | loop fusion | flops 51355136 | bytes 51480576 | tf_op jit(solution)/shard_map/reduce_sum | solution.py:13
  24.5 21.0 %fusion.9 = f32[512,49]{0,1:T(8,128)S(1)} fusion(bf16[512,49,1024]{2,0,1:T(8,128)(2,1)} %param.6, f32[512,49]{0,1:T(8,128)S(1)} %broadcast_multiply_fusion.1), kind=kLoop, calls=%fused_computation.11 | loop fusion | flops 102735360 | bytes 51580928 | tf_op jit(solution)/shard_map/reduce_sum | solution.py:15
  45.5 0.0 copy-start.1
  45.5 0.0 copy-start.4
  45.5 19.5 %fusion.4 = f32[512,1024]{1,0:T(8,128)S(1)} fusion(bf16[512,49,1024]{2,0,1:T(8,128)(2,1)} %param.6, f32[512,49]{0,1:T(8,128)S(1)} %add_rsqrt_fusion, f32[512,49]{0,1:T(8,128)S(1)} %broadcast_multiply_fusion.1), kind=kLoop, calls=%fused_computation.6 | loop fusion | flops 102236160 | bytes 53678080 | tf_op jit(solution)/shard_map/reduce_sum | solution.py:18
  65.0 0.0 copy-done.1
  65.0 0.0 copy-done.4
  65.0 0.0 copy-start.3
  65.1 21.7 %fusion.24 = (f32[512]{0:T(512)S(1)}, f32[512,11264]{1,0:T(8,128)}) fusion(f32[11264]{0:T(1024)S(1)} %copy-done.4, bf16[1024,11264]{1,0:T(8,128)(2,1)} %param.9, f32[512,1024]{1,0:T(8,128)S(1)} %fusion.4, f32[1024]{0:T(1024)S(1)} %copy-done.1, f32[1024]{0:T(1024)S(1)} %broadcast_multiply_fusion.2, pred[11264]{0:T(1024)(128)(4,1)S(1)} %broadcast_compare_fusion), kind=kOutput, calls=%fused_computation.46 | convolution fusion | flops 11830034432 | bytes 48301056 | tf_op jit(solution)/shard_map/dot_general | solution.py:43
  86.7 6.2 pmax.7
  92.9 0.0 copy-done.3
  92.9 12.7 %fusion.14 = (f32[512]{0:T(512)S(1)}, f32[512]{0:T(512)S(1)}, f32[512]{0:T(512)S(1)}) fusion(f32[512,11264]{1,0:T(8,128)} %get-tuple-element.25, f32[512]{0:T(512)S(1)} %pmax.7, pred[11264]{0:T(1024)(128)(4,1)S(1)} %broadcast_compare_fusion, s32[512]{0:T(512)S(1)} %copy-done.3, s32[11264]{0:T(1024)S(1)} %iota_add_fusion), kind=kLoop, calls=%fused_computation.21 | loop fusion | flops 40368640 | bytes 23135232 | tf_op jit(solution)/shard_map/reduce_sum | solution.py:48
  105.6 5.0 psum.49
  110.6 16.8 %fusion.21 = (f32[11264]{0:T(1024)S(1)}, bf16[512,11264]{1,0:T(8,128)(2,1)}) fusion(f32[11264]{0:T(1024)S(1)} %broadcast_select_fusion, s32[512]{0:T(512)S(1)} %copy-done.3, s32[11264]{0:T(1024)S(1)} %iota_add_fusion, f32[512]{0:T(512)S(1)} %bitcast.10, f32[512,11264]{1,0:T(8,128)} %get-tuple-element.25, f32[512]{0:T(512)S(1)} %pmax.7), kind=kLoop, calls=%fused_computation.44 | loop fusion | flops 51893248 | bytes 34744320 | tf_op jit(solution)/shard_map/reduce_sum | solution.py:56
  127.4 19.8 %fusion.17 = f32[512,1024]{1,0:T(8,128)} fusion(bf16[1024,11264]{1,0:T(8,128)(2,1)} %param.9, bf16[512,11264]{1,0:T(8,128)(2,1)} %get-tuple-element.18), kind=kOutput, calls=%fused_computation.24 | convolution fusion | flops 11811160064 | bytes 36700160 | tf_op jit(solution)/shard_map/dot_general | solution.py:57
  147.2 0.0 all-reduce.4.cloned.1.call-update
  147.2 0.0 all-reduce.6.cloned.1.call-start
  147.2 23.4 %fusion.15 = f32[1024,11264]{1,0:T(8,128)} fusion(bf16[512,11264]{1,0:T(8,128)(2,1)} %get-tuple-element.18, f32[512,1024]{1,0:T(8,128)S(1)} %fusion.4, f32[1024]{0:T(1024)S(1)} %copy-done.1, f32[1024]{0:T(1024)S(1)} %broadcast_multiply_fusion.2), kind=kOutput, calls=%fused_computation.22 | convolution fusion | flops 11812732928 | bytes 59777024 | tf_op jit(solution)/shard_map/dot_general | solution.py:55
  170.6 0.0 all-reduce.6.cloned.1.call-update
  170.7 0.6 subtract_reduce_fusion
  171.3 36.5 %all-reduce.4.cloned.1.call-done = f32[512,1024]{1,0:T(8,128)} async-done(((f32[512,1024]{1,0:T(8,128)}), f32[512,1024]{1,0:T(8,128)}) %all-reduce.4.cloned.1.call-update) | async-done | bytes 2097168 | tf_op jit(solution)/shard_map/psum | solution.py:58
  207.8 0.0 copy-done.2
  207.8 3.4 fusion.20
  211.2 26.6 %all-reduce = (f32[]{:T(128)}, f32[11264]{0:T(1024)}, f32[1024]{0:T(1024)}, f32[1024]{0:T(1024)}) all-reduce(f32[]{:T(128)} %subtract_reduce_fusion, f32[11264]{0:T(1024)S(1)} %get-tuple-element.17, f32[1024]{0:T(1024)S(1)} %get-tuple-element.19, f32[1024]{0:T(1024)S(1)} %get-tuple-element.20), channel_id=1, replica_groups=mesh['tp'=2,'dp'=8] {'dp'}, use_global_device_ids=true, to_apply=%region_10.11 | all-reduce | flops 13313 | bytes 106504 | tf_op jit(solution)/shard_map/psum | solution.py:60
  238.4 0.0 copy-start
  238.4 28.1 %fusion.5 = f32[512,49]{0,1:T(8,128)S(1)} fusion(bf16[512,49,1024]{2,0,1:T(8,128)(2,1)} %param.6, f32[512,1024]{1,0:T(8,128)} %get-tuple-element.16, f32[512,49]{0,1:T(8,128)S(1)} %add_rsqrt_fusion, f32[512,49]{0,1:T(8,128)S(1)} %broadcast_multiply_fusion.1), kind=kLoop, calls=%fused_computation.7 | loop fusion | flops 128425472 | bytes 53778432 | tf_op jit(solution)/shard_map/reduce_sum | solution.py:29
  266.6 1.6 broadcast_subtract_fusion
  268.1 36.7 %fusion.8 = bf16[512,49,1024]{2,0,1:T(8,128)(2,1)} fusion(bf16[512,49,1024]{2,0,1:T(8,128)(2,1)} %param.6, f32[512,49]{0,1:T(8,128)S(1)} %broadcast_multiply_fusion, f32[512,1024]{1,0:T(8,128)} %broadcast_subtract_fusion, f32[512,49]{0,1:T(8,128)S(1)} %add_rsqrt_fusion, f32[512,49]{0,1:T(8,128)S(1)} %broadcast_multiply_fusion.1), kind=kLoop, calls=%fused_computation.10 | loop fusion | flops 179830784 | bytes 105158656 | tf_op jit(solution)/shard_map/convert_element_type | solution.py:31
  304.9 434.6 %all-reduce.6.cloned.1.call-done = f32[1024,11264]{1,0:T(8,128)} async-done(((f32[1024,11264]{1,0:T(8,128)}), f32[1024,11264]{1,0:T(8,128)}) %all-reduce.6.cloned.1.call-update) | async-done | bytes 46137360 | tf_op jit(solution)/shard_map/psum | solution.py:55
  739.4 33.7 %copy.14 = f32[1024,11264]{1,0:T(8,128)} copy(f32[1024,11264]{1,0:T(8,128)} %all-reduce.6.cloned.1.call-done) | data formatting | bytes 92274688
  (11 shorter events, 0.1 us)
Async XLA Ops:
  7.2 200.6 %all-reduce.4.cloned.1.call-start = ((), (), s32[]{:S(2)}) async-start(), calls=%async_computation | async-start | bytes 4194304 | tf_op jit(solution)/shard_map/psum | solution.py:58
  45.5 19.5 %copy-start.1 = (f32[1024]{0:T(1024)S(1)}, f32[1024]{0:T(1024)}, u32[]{:S(2)}) copy-start(f32[1024]{0:T(1024)} %param.8) | copy-start | bytes 12292
  45.5 19.5 %copy-start.4 = (f32[11264]{0:T(1024)S(1)}, f32[11264]{0:T(1024)}, u32[]{:S(2)}) copy-start(f32[11264]{0:T(1024)} %param.10) | copy-start | bytes 135172
  65.0 27.9 %copy-start.3 = (s32[512]{0:T(512)S(1)}, s32[512]{0:T(512)}, u32[]{:S(2)}) copy-start(s32[512]{0:T(512)} %param.11) | copy-start | bytes 6148
  147.2 592.2 %all-reduce.6.cloned.1.call-start = ((), (), s32[]{:S(2)}) async-start(), calls=%async_computation.1 | async-start | bytes 92274688 | tf_op jit(solution)/shard_map/psum | solution.py:55
  170.6 37.2 %copy-start.2 = (f32[1024]{0:T(1024)S(1)}, f32[1024]{0:T(1024)}, u32[]{:S(2)}) copy-start(f32[1024]{0:T(1024)} %param.7) | copy-start | bytes 12292
  238.4 28.1 %copy-start = (f32[512,1024]{1,0:T(8,128)S(1)}, f32[512,1024]{1,0:T(8,128)}, u32[]{:S(2)}) copy-start(f32[512,1024]{1,0:T(8,128)} %get-tuple-element.16) | copy-start | bytes 6291460
Sparse Core Ops, SparseCore 0:
  147.3 60.4 all-reduce.3
  212.2 527.2 all-reduce.5
where the time goes:
time: 782 us; the launch traced here: 781 us
  waiting for transfers between devices  471 us (60%)
  other arithmetic  158 us (20%)
  matrix products  64.8 us (8%)
  blocking collectives  37.8 us (5%)
  local copies, waits for them, and re-layouts  33.7 us (4%)
  between operations  16 us (2%)
    psum x1, waiting for transfers between devices, local_head(): lax.psum(lax.dot_general(pooled16, dlogit16, (((0,), (0,)), ((), ())), pr...  435 us
    convert_element_type x1, other arithmetic, norm_backward(): return (grad_x.astype(jnp.bfloat16), grad_gamma, grad_beta)  36.7 us
    psum x1, waiting for transfers between devices, local_head(): grad_pool = lax.psum(grad_pool, 'tp')  36.5 us
    unnamed x11, local copies, waits for them, and re-layouts  33.7 us
    reduce_sum x1, other arithmetic, norm_backward(): proj_term = jnp.mean(x_hat * upstream[:, None, :], axis=-1, keepdims=True)  28.1 us
    psum x1, blocking collectives, local_head(): lax.psum((jnp.sum(loss_rows), grad_gamma, grad_beta), 'dp')  26.6 us
    dot_general x1, matrix products, local_head(): lax.dot_general(pooled16, dlogit16, (((0,), (0,)), ((), ())), preferred_e...  23.4 us
    dot_general x1, matrix products, local_head(): jnp.dot(pooled16, w_head, preferred_element_type=jnp.float32) + b_head  21.7 us
  transfers between devices with their start and end apart: 2, of which 2 were waited for; matrix products, arithmetic and copies ran while one was open for 12% of the time, Pallas kernels for 0%

commit v1 on v0

v1 whole, which is shorter than its diff:
```python
import functools

import jax
import jax.numpy as jnp
from jax import lax
from jax.experimental import pallas as pl
from jax.experimental.pallas import tpu as pltpu
from jax.sharding import PartitionSpec as P


VALID = 21841
LN_EPS = 1e-5
SMOOTH = 0.1
F32 = jnp.float32
BF16 = jnp.bfloat16
MIB = 2**20


def _cost(flops, nbytes):
    return pl.CostEstimate(flops=int(flops), bytes_accessed=int(nbytes), transcendentals=0)


def _ln_kernel(f_ref, g_ref, b_ref, p_ref, xm_ref, mean_ref, inv_ref, *, rows, sub, group):
    lane = lax.broadcasted_iota(jnp.int32, (sub, 128), 1)
    tokens, _, width = f_ref.shape
    ones = jnp.ones((width, 128), BF16)

    def step(s, carry):
        r = pl.ds(pl.multiple_of(s * sub, sub), sub)
        acc = jnp.zeros((sub, width), F32)
        means = jnp.zeros((sub, 128), F32)
        invs = jnp.zeros((sub, 128), F32)
        for t0 in range(0, tokens, group):
            xb = f_ref[t0 : t0 + group, r, :].reshape(group * sub, width)
            mu_all = jnp.dot(xb, ones, preferred_element_type=F32) * (1.0 / width)
            mus, ivs = [], []
            for j in range(group):
                mu = mu_all[j * sub : (j + 1) * sub, :]
                x = f_ref[t0 + j, r, :].astype(F32)
                q = jnp.zeros((sub, 128), F32)
                for k in range(width // 128):
                    d = x[:, k * 128 : (k + 1) * 128] - mu
                    q = q + d * d
                var = jnp.sum(q, -1, keepdims=True) * (1.0 / width)
                mus.append(mu)
                ivs.append(lax.rsqrt(var + LN_EPS))
            for j in range(group):
                x = f_ref[t0 + j, r, :].astype(F32)
                hats = [(x[:, k * 128 : (k + 1) * 128] - mus[j]) * ivs[j] for k in range(width // 128)]
                acc = acc + jnp.concatenate(hats, 1)
                hit = lane == t0 + j
                means = jnp.where(hit, mus[j], means)
                invs = jnp.where(hit, ivs[j], invs)
        xm = acc * (1.0 / tokens)
        xm_ref[r, :] = xm
        p_ref[r, :] = (xm * g_ref[...] + b_ref[...]).astype(BF16).astype(F32)
        mean_ref[r, :] = means
        inv_ref[r, :] = invs
        return carry

    lax.fori_loop(0, rows // sub, step, 0)


def _ln_forward(ft, gamma, beta, rows=32, sub=32, group=7):
    tokens, images, width = ft.shape
    return pl.pallas_call(
        functools.partial(_ln_kernel, rows=rows, sub=sub, group=group),
        grid=(images // rows,),
        in_specs=[
            pl.BlockSpec((tokens, rows, width), lambda i: (0, i, 0)),
            pl.BlockSpec((1, width), lambda i: (0, 0)),
            pl.BlockSpec((1, width), lambda i: (0, 0)),
        ],
        out_specs=[pl.BlockSpec((rows, width), lambda i: (i, 0))] * 2 + [pl.BlockSpec((rows, 128), lambda i: (i, 0))] * 2,
        out_shape=[jax.ShapeDtypeStruct((images, width), F32)] * 2 + [jax.ShapeDtypeStruct((images, 128), F32)] * 2,
        compiler_params=pltpu.CompilerParams(vmem_limit_bytes=60 * MIB),
        cost_estimate=_cost(36e-6 * 996e12, tokens * images * width * 2),
        name="ln_forward",
    )(ft, gamma, beta)


def _df_kernel(f_ref, da_ref, db_ref, g_ref, mean_ref, inv_ref, o_ref, *, rows, sub, group):
    tokens, _, width = f_ref.shape

    def step(s, carry):
        r = pl.ds(pl.multiple_of(s * sub, sub), sub)
        up = (da_ref[r, :] + db_ref[r, :]) * g_ref[...] * (1.0 / tokens)
        up = up - jnp.mean(up, -1, keepdims=True)
        means = mean_ref[r, :]
        invs = inv_ref[r, :]
        for t0 in range(0, tokens, group):
            mus, ivs, ks = [], [], []
            for t in range(t0, t0 + group):
                mu, iv = means[:, t : t + 1], invs[:, t : t + 1]
                x = f_ref[t, r, :].astype(F32)
                q = jnp.zeros((sub, 128), F32)
                for k in range(width // 128):
                    c = slice(k * 128, (k + 1) * 128)
                    q = q + (x[:, c] - mu) * up[:, c]
                proj = jnp.sum(q, -1, keepdims=True) * (1.0 / width)
                mus.append(mu)
                ivs.append(iv)
                ks.append(proj * iv * iv * iv)
            for j in range(group):
                x = f_ref[t0 + j, r, :].astype(F32)
                o_ref[t0 + j, r, :] = (ivs[j] * up - (x - mus[j]) * ks[j]).astype(BF16)
        return carry

    lax.fori_loop(0, rows // sub, step, 0)


def _ln_backward(ft, dpool_a, dpool_b, gamma, means, invs, rows=32, sub=32, group=7):
    tokens, images, width = ft.shape
    row_block = pl.BlockSpec((rows, width), lambda i: (i, 0))
    stat_block = pl.BlockSpec((rows, 128), lambda i: (i, 0))
    return pl.pallas_call(
        functools.partial(_df_kernel, rows=rows, sub=sub, group=group),
        grid=(images // rows,),
        in_specs=[
            pl.BlockSpec((tokens, rows, width), lambda i: (0, i, 0)),
            row_block,
            row_block,
            pl.BlockSpec((1, width), lambda i: (0, 0)),
            stat_block,
            stat_block,
        ],
        out_specs=pl.BlockSpec((tokens, rows, width), lambda i: (0, i, 0)),
        out_shape=jax.ShapeDtypeStruct((tokens, images, width), BF16),
        compiler_params=pltpu.CompilerParams(vmem_limit_bytes=60 * MIB),
        cost_estimate=_cost(45e-6 * 996e12, tokens * images * width * 4),
        name="ln_backward",
    )(ft, dpool_a, dpool_b, gamma, means, invs)


def _logits_kernel(base_ref, p_ref, w_ref, b_ref, y_ref, l_ref, st_ref, m_acc, s_acc, t_acc, v_acc, p16, *, tile, row_block):
    i = pl.program_id(0)

    @pl.when(i == 0)
    def _():
        m_acc[...] = jnp.full(m_acc.shape, -jnp.inf, F32)
        for acc in (s_acc, t_acc, v_acc):
            acc[...] = jnp.zeros(acc.shape, F32)
        p16[...] = p_ref[...].astype(BF16)

    col = base_ref[0] + i * tile + lax.broadcasted_iota(jnp.int32, (1, tile), 1)
    valid = col < VALID
    groups = [slice(k * 128, (k + 1) * 128) for k in range(tile // 128)]
    for r0 in range(0, p16.shape[0], row_block):
        r = slice(r0, r0 + row_block)
        raw = jnp.dot(p16[r, :], w_ref[...], preferred_element_type=F32) + b_ref[...]
        logit = jnp.where(valid, raw, -1e30)
        l_ref[r, :] = logit
        target = jnp.where(col == y_ref[r, :], logit, 0.0)
        kept = jnp.where(valid, raw, 0.0)
        m0 = m_acc[r, :]
        m = m0
        for g in groups:
            m = jnp.maximum(m, logit[:, g])
        s = s_acc[r, :] * jnp.exp(m0 - m)
        t, v = t_acc[r, :], v_acc[r, :]
        for g in groups:
            s = s + jnp.exp(logit[:, g] - m)
            t = t + target[:, g]
            v = v + kept[:, g]
        m_acc[r, :] = m
        s_acc[r, :] = s
        t_acc[r, :] = t
        v_acc[r, :] = v

    @pl.when(i == pl.num_programs(0) - 1)
    def _():
        m = m_acc[...]
        top = jnp.max(m, -1, keepdims=True)
        norm = jnp.sum(s_acc[...] * jnp.exp(m - top), -1, keepdims=True)
        target = jnp.sum(t_acc[...], -1, keepdims=True)
        total = jnp.sum(v_acc[...], -1, keepdims=True)
        lane = lax.broadcasted_iota(jnp.int32, (1, 128), 1)
        st_ref[...] = jnp.where(lane == 0, top, jnp.where(lane == 1, norm, jnp.where(lane == 2, target, total)))


def _own_logits(base, p, w, b, y, tile=1024, row_block=256):
    images, width = p.shape
    cols = w.shape[1]
    return pl.pallas_call(
        functools.partial(_logits_kernel, tile=tile, row_block=row_block),
        grid_spec=pltpu.PrefetchScalarGridSpec(
            num_scalar_prefetch=1,
            grid=(cols // tile,),
            in_specs=[
                pl.BlockSpec((images, width), lambda i, s: (0, 0)),
                pl.BlockSpec((width, tile), lambda i, s: (0, i)),
                pl.BlockSpec((1, tile), lambda i, s: (0, i)),
                pl.BlockSpec((images, 1), lambda i, s: (0, 0)),
            ],
            out_specs=[pl.BlockSpec((images, tile), lambda i, s: (0, i)), pl.BlockSpec((images, 128), lambda i, s: (0, 0))],
            scratch_shapes=[pltpu.VMEM((images, 128), F32)] * 4 + [pltpu.VMEM((images, width), BF16)],
        ),
        out_shape=[jax.ShapeDtypeStruct((images, cols), F32), jax.ShapeDtypeStruct((images, 128), F32)],
        compiler_params=pltpu.CompilerParams(vmem_limit_bytes=56 * MIB),
        cost_estimate=_cost(2 * images * width * cols, width * cols * 2 + images * cols * 4),
        name="own_logits",
    )(base, p, w, b, y)


def _dlogit(logit, shift, col, y, total):
    flat = SMOOTH / VALID / total
    drop = jnp.where(col == y, flat + (1.0 - SMOOTH) / total, flat)
    return jnp.where(col < VALID, jnp.exp(logit - shift) - drop, 0.0)


def _dpool_kernel(base_ref, l_ref, w_ref, shift_ref, y_ref, o_ref, *, tile, total):
    i = pl.program_id(0)
    col = base_ref[0] + i * tile + lax.broadcasted_iota(jnp.int32, (1, tile), 1)
    d = _dlogit(l_ref[...], shift_ref[...], col, y_ref[...], total).astype(BF16)
    part = lax.dot_general(d, w_ref[...], (((1,), (1,)), ((), ())), preferred_element_type=F32)

    @pl.when(i == 0)
    def _():
        o_ref[...] = part

    @pl.when(i > 0)
    def _():
        o_ref[...] += part


def _own_dpool(base, logits, w, shift, y, total, tile=1024):
    images, cols = logits.shape
    width = w.shape[0]
    column = pl.BlockSpec((images, 1), lambda i, s: (0, 0))
    return pl.pallas_call(
        functools.partial(_dpool_kernel, tile=tile, total=total),
        grid_spec=pltpu.PrefetchScalarGridSpec(
            num_scalar_prefetch=1,
            grid=(cols // tile,),
            in_specs=[
                pl.BlockSpec((images, tile), lambda i, s: (0, i)),
                pl.BlockSpec((width, tile), lambda i, s: (0, i)),
                column,
                column,
            ],
            out_specs=pl.BlockSpec((images, width), lambda i, s: (0, 0)),
        ),
        out_shape=jax.ShapeDtypeStruct((images, width), F32),
        compiler_params=pltpu.CompilerParams(vmem_limit_bytes=56 * MIB),
        cost_estimate=_cost(2 * images * width * cols, width * cols * 2 + images * cols * 4),
        name="own_dpool",
    )(base, logits, w, shift, y)


def _dw_kernel(sc_ref, *refs, counts, tile, row_block, total, has_acc, to_full, aliased, own, off):
    refs = list(refs)
    take = lambda n: [refs.pop(0) for _ in range(n)]
    p_refs = take(len(counts))
    w_ref, b_ref, shift_ref, y_ref = take(4)
    acc_ref, acc_db_ref = take(2) if has_acc else (None, None)
    got_ref = None
    if aliased:
        _, = take(1)
        if aliased > 1:
            got_ref, = take(1)
    full_ref, = take(1) if to_full else (None,)
    o_ref, db_ref = take(2)
    p16, d16 = refs
    i = pl.program_id(0)

    @pl.when(i == 0)
    def _():
        r0 = 0
        for ref, n in zip(p_refs, counts):
            p16[r0 : r0 + n, :] = ref[...].astype(BF16)
            r0 += n

    def compute():
        col = sc_ref[0] + (off + i) * tile + lax.broadcasted_iota(jnp.int32, (1, tile), 1)
        db = jnp.zeros((1, tile), F32)
        for r0 in range(0, p16.shape[0], row_block):
            r = slice(r0, r0 + row_block)
            logit = jnp.dot(p16[r, :], w_ref[...], preferred_element_type=F32) + b_ref[...]
            d = _dlogit(logit, shift_ref[r, :], col, y_ref[r, :], total)
            db = db + jnp.sum(d, 0, keepdims=True)
            d16[r, :] = d.astype(BF16)
        out = lax.dot_general(p16[...], d16[...], (((0,), (0,)), ((), ())), preferred_element_type=F32)
        if has_acc:
            out = out + acc_ref[...]
            db = db + acc_db_ref[...]
        o_ref[...] = out
        if to_full:
            full_ref[...] = out
        db_ref[...] = db

    if got_ref is None:
        compute()
    else:
        pl.when(i < own)(compute)

        @pl.when(i >= own)
        def _():
            full_ref[...] = got_ref[...]


def _dw_phase(sc, pooled, w, b, shift, y, total, acc=None, own=None, off=0, full=None, got=None, got_off=0, to_full=False, tile=512, row_block=256):
    counts = [p.shape[0] for p in pooled]
    images = sum(counts)
    width, cols = w.shape
    own = own or cols // 2 // tile
    extra = got.shape[1] // tile if got is not None else 0
    mine = lambda i: jnp.minimum(i, own - 1)
    theirs = lambda i: jnp.maximum(i - own, 0)
    in_specs = [pl.BlockSpec(p.shape, lambda i, s: (0, 0)) for p in pooled]
    in_specs += [
        pl.BlockSpec((width, tile), lambda i, s: (0, s[1] + off + mine(i))),
        pl.BlockSpec((1, tile), lambda i, s: (0, s[1] + off + mine(i))),
        pl.BlockSpec((images, 1), lambda i, s: (0, 0)),
        pl.BlockSpec((images, 1), lambda i, s: (0, 0)),
    ]
    args = list(pooled) + [w, b, shift, y]
    if acc is not None:
        in_specs += [pl.BlockSpec((width, tile), lambda i, s: (0, off + mine(i))), pl.BlockSpec((1, tile), lambda i, s: (0, off + mine(i)))]
        args += list(acc)
    aliases = {}
    aliased = 0
    if full is not None:
        aliased = 1
        aliases = {len(args) + 1: 0}
        in_specs.append(pl.BlockSpec(memory_space=pl.ANY))
        args.append(full)
    if got is not None:
        aliased = 2
        in_specs.append(pl.BlockSpec((width, tile), lambda i, s: (0, theirs(i))))
        args.append(got)
    out_specs = [pl.BlockSpec((width, tile), lambda i, s: (0, mine(i))), pl.BlockSpec((1, tile), lambda i, s: (0, mine(i)))]
    out_shape = [jax.ShapeDtypeStruct((width, own * tile), F32), jax.ShapeDtypeStruct((1, own * tile), F32)]
    if to_full:
        place = lambda i, s: (0, jnp.where(i < own, s[1] + off + i, s[2] + got_off + i - own))
        out_specs.insert(0, pl.BlockSpec((width, tile), place))
        out_shape.insert(0, jax.ShapeDtypeStruct((width, cols), F32))
    return pl.pallas_call(
        functools.partial(
            _dw_kernel, counts=counts, tile=tile, row_block=row_block, total=total, has_acc=acc is not None, to_full=to_full, aliased=aliased, own=own, off=off
        ),
        grid_spec=pltpu.PrefetchScalarGridSpec(
            num_scalar_prefetch=1,
            grid=(own + extra,),
            in_specs=in_specs,
            out_specs=out_specs,
            scratch_shapes=[pltpu.VMEM((images, width), BF16), pltpu.VMEM((images, tile), BF16)],
        ),
        out_shape=out_shape,
        input_output_aliases=aliases,
        compiler_params=pltpu.CompilerParams(vmem_limit_bytes=63 * MIB),
        cost_estimate=_cost(4.6 * images * width * own * tile, width * own * tile * 10),
        name="dw_phase",
    )(sc, *args)


def _place_kernel(sc_ref, full_in, *refs, starts):
    parts, full_ref = refs[:-1], refs[-1]
    i = pl.program_id(0)
    for ref, start, stop in zip(parts, starts[:-1], starts[1:]):

        @pl.when((i >= start) & (i < stop))
        def _():
            full_ref[...] = ref[...]


def _place(sc, full, parts, off, tile=512):
    width, cols = full.shape
    starts = [0]
    for part in parts:
        starts.append(starts[-1] + part.shape[1] // tile)
    specs = [
        pl.BlockSpec((width, tile), lambda i, s, lo=lo, hi=hi: (0, jnp.clip(i - lo, 0, hi - lo - 1))) for lo, hi in zip(starts[:-1], starts[1:])
    ]
    return pl.pallas_call(
        functools.partial(_place_kernel, starts=starts),
        grid_spec=pltpu.PrefetchScalarGridSpec(
            num_scalar_prefetch=1,
            grid=(starts[-1],),
            in_specs=[pl.BlockSpec(memory_space=pl.ANY)] + specs,
            out_specs=pl.BlockSpec((width, tile), lambda i, s: (0, s[2] + off + i)),
        ),
        out_shape=jax.ShapeDtypeStruct((width, cols), F32),
        input_output_aliases={1: 0},
        compiler_params=pltpu.CompilerParams(vmem_limit_bytes=60 * MIB),
        cost_estimate=_cost(6e-6 * 996e12, width * starts[-1] * tile * 8),
        name="place",
    )(sc, full, *parts)


CHUNKS = (3, 3, 3, 2)
TILE = 512


def solution(mesh):
    dp_size, tp_size = mesh.shape["dp"], mesh.shape["tp"]

    def swap(x, bit):
        return lax.ppermute(x, "dp", [(i, i ^ bit) for i in range(dp_size)])

    def head(feats, ln_gamma, ln_beta, w, b, labels):
        images, _, width = feats.shape
        cols = w.shape[1]
        total = images * dp_size
        tp_i, dp_i = lax.axis_index("tp"), lax.axis_index("dp")
        core = dp_i % 2
        half_tiles = cols // 2 // TILE
        base = (tp_i * cols).astype(jnp.int32).reshape(1)
        sc = jnp.stack([tp_i * cols + core * (cols // 2), core * half_tiles, (1 - core) * half_tiles]).astype(jnp.int32)
        ft = jnp.transpose(feats, (1, 0, 2))
        gamma, beta, bias = ln_gamma.reshape(1, width), ln_beta.reshape(1, width), b.reshape(1, cols)
        y_col = labels.reshape(images, 1)

        p, xm, means, invs = _ln_forward(ft, gamma, beta)
        p_core, p_x, p_y = swap(p, 1), swap(p, 2), swap(p, 4)

        logits, st = _own_logits(base, p, w, bias, y_col)
        rows = jnp.concatenate([st[:, :4].T, labels.astype(F32)[None], jnp.zeros((3, images), F32)], 0)
        every = lax.all_gather(rows, ("tp", "dp"))
        every = every.reshape(tp_size, dp_size, 8, images)
        top = jnp.max(every[:, :, 0], 0)
        lse = top + jnp.log(jnp.sum(every[:, :, 1] * jnp.exp(every[:, :, 0] - top), 0))
        target = jnp.sum(every[:, :, 2], 0)
        valid_sum = jnp.sum(every[:, :, 3], 0)
        loss = jnp.sum(lse - (1.0 - SMOOTH) * target - (SMOOTH / VALID) * valid_sum) / total
        shift_all = lse + jnp.log(F32(total))
        y_all = every[0, :, 4].astype(jnp.int32)

        def pick(bits):
            idx = dp_i ^ jnp.array(bits, jnp.int32)
            return shift_all[idx].reshape(-1, 1), y_all[idx].reshape(-1, 1)

        shift_own, _ = pick([0])
        dpool_a = _own_dpool(base, logits, w, shift_own, y_col, total)
        dpool_b = lax.ppermute(dpool_a, "tp", [(i, tp_size - 1 - i) for i in range(tp_size)])

        acc = _dw_phase(sc, [p, p_core], w, bias, *pick([0, 1]), total)
        acc = _dw_phase(sc, [p_x, p_y], w, bias, *pick([2, 4]), total, acc=acc)
        half = images // 2
        p_d = [swap(p_x[:half], 4), swap(p_y[half:], 2)]
        p_rest = [swap(p_x, 1), swap(p_y, 1)] + p_d
        p_rest += [swap(p_d[0], 1), swap(p_d[1], 1)]
        shift_rest, y_rest = pick([3, 5, 6, 7])

        full, sent, dbs, off = None, [], [], 0
        offs = []
        for c, n in enumerate(CHUNKS):
            got = sent[c - 2] if c >= 2 else None
            full, part, db = _dw_phase(
                sc, p_rest, w, bias, shift_rest, y_rest, total, acc=acc, own=n, off=off, full=full, got=got, got_off=offs[c - 2] if c >= 2 else 0, to_full=True
            )
            sent.append(swap(part, 1))
            dbs.append(db)
            offs.append(off)
            off += n

        db_mine = jnp.concatenate(dbs, 1)
        db_other = swap(db_mine, 1)
        grad_b = jnp.where(core == 0, jnp.concatenate([db_mine, db_other], 1), jnp.concatenate([db_other, db_mine], 1)).reshape(cols)

        dpool = dpool_a + dpool_b
        sums = jnp.stack([jnp.sum(dpool * xm, 0), jnp.sum(dpool, 0)])
        for bit in (1, 2, 4):
            sums = sums + swap(sums, bit)

        dft = _ln_backward(ft, dpool_a, dpool_b, gamma, means, invs)
        full = _place(sc, full, sent[-2:], offs[-2])
        return loss, jnp.transpose(dft, (1, 0, 2)), full, grad_b, sums[0], sums[1]

    return jax.shard_map(
        head,
        mesh=mesh,
        in_specs=(P("dp", None, None), P(), P(), P(None, "tp"), P("tp"), P("dp")),
        out_specs=(P(), P("dp", None, None), P(None, "tp"), P("tp"), P(), P()),
        check_vma=False,
    )
```

time: 782 us -> 486 us (0.62)
  waiting for transfers between devices: 471 us -> 52.1 us
  Pallas kernels: 0 us -> 364 us
  other arithmetic: 158 us -> 5.39 us
  matrix products: 64.8 us -> 0 us
  local copies, waits for them, and re-layouts: 33.7 us -> 18.6 us
  between operations: 16 us -> 3.03 us
  blocking collectives: 37.8 us -> 25.4 us
  starting transfers between devices: 0.08 us -> 10.7 us
    psum x2 -> x0, waiting for transfers between devices: 471 us -> none  [the longest x1 435 us: local_head(): lax.psum(lax.dot_general(pooled16, dlogit16, (((0,), (0,)), ((), ())), pr...]
    pallas_call x0 -> x11, Pallas kernels: none -> 364 us  [the longest x6 169 us: _dw_phase(): pl.pallas_call(functools.partial(_dw_kernel, counts=counts, tile=tile, ro...]
    reduce_sum x8 -> x2, other arithmetic: 119 us -> 2.97 us  [the longest x1 2.96 us: head(): sums = jnp.stack([jnp.sum(dpool * xm, 0), jnp.sum(dpool, 0)])]
    dot_general x3 -> x0, matrix products: 64.8 us -> none  [the longest x1 23.4 us: local_head(): lax.dot_general(pooled16, dlogit16, (((0,), (0,)), ((), ())), preferred_e...]
    ppermute x0 -> x18, waiting for transfers between devices: none -> 52.1 us  [the longest x1 47.3 us: head(): lax.ppermute(dpool_a, 'tp', [(i, tp_size - 1 - i) for i in range(tp_size)])]
    convert_element_type x1 -> x2, other arithmetic: 36.7 us -> 0.01 us  [the longest x1 0.01 us: head(): y_all = every[0, :, 4].astype(jnp.int32)]
    psum x2 -> x0, blocking collectives: 31.6 us -> none  [the longest x1 26.6 us: local_head(): lax.psum((jnp.sum(loss_rows), grad_gamma, grad_beta), 'dp')]
    unnamed x11 -> x38, local copies, waits for them, and re-layouts: 33.7 us -> 7.05 us
  transfers between devices with their start and end apart: 2 -> 18, of which waited for: 2 -> 4; matrix products, arithmetic and copies ran while one was open for 12% -> 5% of each run, Pallas kernels for 0% -> 60%
where the time goes in v1:
time: 486 us; the launch traced here: 480 us
  Pallas kernels  364 us (75%)
  waiting for transfers between devices  52.1 us (11%)
  blocking collectives  25.4 us (5%)
  local copies, waits for them, and re-layouts  18.6 us (4%)
  starting transfers between devices  10.7 us (2%)
  other arithmetic  5.39 us (1%)
    pallas_call x6, Pallas kernels, _dw_phase(): pl.pallas_call(functools.partial(_dw_kernel, counts=counts, tile=tile, ro...  169 us
    pallas_call x1, Pallas kernels, _ln_backward(): pl.pallas_call(functools.partial(_df_kernel, rows=rows, sub=sub, group=gr...  92.2 us
    ppermute x1, waiting for transfers between devices, head(): lax.ppermute(dpool_a, 'tp', [(i, tp_size - 1 - i) for i in range(tp_size)])  47.3 us
    pallas_call x1, Pallas kernels, _ln_forward(): pl.pallas_call(functools.partial(_ln_kernel, rows=rows, sub=sub, group=gr...  40.5 us
    pallas_call x1, Pallas kernels, _own_logits(): pl.pallas_call(functools.partial(_logits_kernel, tile=tile, row_block=row...  27 us
    all_gather x1, blocking collectives, head(): every = lax.all_gather(rows, ('tp', 'dp'))  25.4 us
    pallas_call x1, Pallas kernels, _own_dpool(): pl.pallas_call(functools.partial(_dpool_kernel, tile=tile, total=total),...  24.6 us
    pallas_call x1, Pallas kernels, _place(): pl.pallas_call(functools.partial(_place_kernel, starts=starts), grid_spec...  11 us
  transfers between devices with their start and end apart: 18, of which 4 were waited for; matrix products, arithmetic and copies ran while one was open for 5% of the time, Pallas kernels for 60%

profile of v1, /device:TPU:0, one launch (start us, length us, event | category | flops | bytes accessed | tf_op | source)
XLA Modules:
  0.0 479.6 jit_solution(8485717099171194260)
XLA Ops:
  0.6 40.5 %ln_forward.1 = (f32[512,1024]{1,0:T(8,128)}, f32[512,1024]{1,0:T(8,128)}, f32[512,128]{1,0:T(8,128)}, f32[512,128]{1,0:T(8,128)}) custom-call(bf16[49,512,1024]{2,1,0:T(8,128)(2,1)} %bitcast.104, f32[1,1024]{1,0:T(1,128)} %bitcast.107, f32[1,1024]{1,0:T(1,128)} %bitcast.106), custom_call_target="tpu_custom_call" | custom-call | flops 35855998976 | bytes 51380224 | tf_op jit(solution)/shard_map/ln_forward/pallas_call | solution.py:66
  41.1 0.8 collective-permute-start.9
  41.9 2.5 collective-permute-start.1
  44.4 1.5 collective-permute-start.3
  45.9 0.9 copy.41.y_ref
  46.8 27.0 %own_logits.1 = (f32[512,11264]{1,0:T(8,128)}, f32[512,128]{1,0:T(8,128)}) custom-call(s32[1]{0:T(128)} %bitcast.base_ref, f32[512,1024]{1,0:T(8,128)} %get-tuple-element.28.p_ref.refs_0_, bf16[1024,11264]{1,0:T(8,128)(2,1)} %refs_6_.7, f32[1,11264]{1,0:T(1,128)} %bitcast.67, s32[512,1]{1,0:T(8,128)} %copy.41.y_ref), custom_call_target="tpu_custom_call" | custom-call | flops 11811160064 | bytes 46137344 | tf_op jit(solution)/shard_map/own_logits/pallas_call | solution.py:184
  73.8 1.0 slice_bitcast_fusion
  75.1 25.4 %all-gather = f32[128,512]{1,0:T(8,128)S(1)} all-gather(f32[8,512]{1,0:T(8,128)S(1)} %maximum_maximum_fusion), channel_id=2, replica_groups=mesh['tp'=2,'dp'=8] {'tp','dp'}, dimensions={0}, use_global_device_ids=true | all-gather | bytes 278528 | tf_op jit(solution)/shard_map/all_gather | solution.py:418
  104.8 1.0 copy.70
  105.9 1.0 copy.72
  106.9 1.1 copy.66
  108.0 1.0 copy.68
  109.0 1.3 copy.62
  110.4 1.4 copy.64
  112.5 2.3 slice.64
  115.3 2.3 slice.65
  117.6 1.5 collective-permute-start.6
  119.6 35.1 %dw_phase.6 = (f32[1024,5632]{1,0:T(8,128)}, f32[1,5632]{1,0:T(1,128)}) custom-call(s32[3]{0:T(128)} %pad_add_fusion.sc_ref, f32[512,1024]{1,0:T(8,128)} %get-tuple-element.28.p_ref.refs_0_, f32[512,1024]{1,0:T(8,128)} %collective-permute-done.9.refs_1_, bf16[1024,11264]{1,0:T(8,128)(2,1)} %refs_6_.7, f32[1,11264]{1,0:T(1,128)} %bitcast.68, ...), custom_call_target="tpu_custom_call" | custom-call | flops 27165667328 | bytes 57671680 | tf_op jit(solution)/shard_map/dw_phase/pallas_call | solution.py:337
  155.2 35.5 %dw_phase.7 = (f32[1024,5632]{1,0:T(8,128)}, f32[1,5632]{1,0:T(1,128)}) custom-call(s32[3]{0:T(128)} %pad_add_fusion.sc_ref, f32[512,1024]{1,0:T(8,128)} %collective-permute-done.1.refs_0_, f32[512,1024]{1,0:T(8,128)} %collective-permute-done.3.refs_1_, bf16[1024,11264]{1,0:T(8,128)(2,1)} %refs_6_.7, f32[1,11264]{1,0:T(1,128)} %bitcast.69, ...), custom_call_target="tpu_custom_call" | custom-call | flops 27165667328 | bytes 57671680 | tf_op jit(solution)/shard_map/dw_phase/pallas_call | solution.py:337
  190.7 23.5 %dw_phase.8 = (f32[1024,11264]{1,0:T(8,128)}, f32[1024,1536]{1,0:T(8,128)}, f32[1,1536]{1,0:T(1,128)}) custom-call(s32[3]{0:T(128)} %pad_add_fusion.sc_ref, f32[512,1024]{1,0:T(8,128)} %collective-permute-done.2.refs_0_, f32[512,1024]{1,0:T(8,128)} %collective-permute-done.4.refs_1_, f32[256,1024]{1,0:T(8,128)} %collective-permute-done.5.refs_2_, ...), custom_call_target="tpu_custom_call" | custom-call | flops 14817637376 | bytes 15728640 | tf_op jit(solution)/shard_map/dw_phase/pallas_call | solution.py:337
  214.3 23.7 %dw_phase.9 = (f32[1024,11264]{1,0:T(8,128)}, f32[1024,1536]{1,0:T(8,128)}, f32[1,1536]{1,0:T(1,128)}) custom-call(s32[3]{0:T(128)} %pad_add_fusion.sc_ref, f32[512,1024]{1,0:T(8,128)} %collective-permute-done.2.refs_0_, f32[512,1024]{1,0:T(8,128)} %collective-permute-done.4.refs_1_, ...), custom_call_target="tpu_custom_call", output_to_operand_aliasing={{0}: (13, {})} | custom-call | flops 14817637376 | bytes 15728640 | tf_op jit(solution)/shard_map/dw_phase/pallas_call | solution.py:337
  238.5 0.9 copy.43.shift_ref
  239.4 24.6 %own_dpool.1.da_ref = f32[512,1024]{1,0:T(8,128)} custom-call(s32[1]{0:T(128)} %bitcast.base_ref, f32[512,11264]{1,0:T(8,128)} %get-tuple-element.30.l_ref, bf16[1024,11264]{1,0:T(8,128)(2,1)} %refs_6_.7, f32[512,1]{1,0:T(8,128)} %copy.43.shift_ref, s32[512,1]{1,0:T(8,128)} %copy.41.y_ref), custom_call_target="tpu_custom_call" | custom-call | flops 11811160064 | bytes 46137344 | tf_op jit(solution)/shard_map/own_dpool/pallas_call | solution.py:230
  264.4 47.3 %collective-permute-done.db_ref = f32[512,1024]{1,0:T(8,128)S(1)} collective-permute-done((f32[512,1024]{1,0:T(8,128)}, f32[512,1024]{1,0:T(8,128)S(1)}, u32[]{:S(2)}, u32[]{:S(2)}) %collective-permute-start) | collective-permute-done | bytes 2097184 | tf_op jit(solution)/shard_map/ppermute | solution.py:434
  311.7 3.0 multiply_reduce_fusion
  314.8 1.2 collective-permute-done.15
  317.2 2.5 collective-permute-done.16
  320.2 28.1 %dw_phase.10 = (f32[1024,11264]{1,0:T(8,128)}, f32[1024,1536]{1,0:T(8,128)}, f32[1,1536]{1,0:T(1,128)}) custom-call(s32[3]{0:T(128)} %pad_add_fusion.sc_ref, f32[512,1024]{1,0:T(8,128)} %collective-permute-done.2.refs_0_, f32[512,1024]{1,0:T(8,128)} %collective-permute-done.4.refs_1_, ...), custom_call_target="tpu_custom_call", output_to_operand_aliasing={{0}: (13, {})} | custom-call | flops 14817637376 | bytes 15728640 | tf_op jit(solution)/shard_map/dw_phase/pallas_call | solution.py:337
  348.4 23.3 %dw_phase.11 = (f32[1024,11264]{1,0:T(8,128)}, f32[1024,1024]{1,0:T(8,128)}, f32[1,1024]{1,0:T(1,128)}) custom-call(s32[3]{0:T(128)} %pad_add_fusion.sc_ref, f32[512,1024]{1,0:T(8,128)} %collective-permute-done.2.refs_0_, f32[512,1024]{1,0:T(8,128)} %collective-permute-done.4.refs_1_, ...), custom_call_target="tpu_custom_call", output_to_operand_aliasing={{0}: (13, {})} | custom-call | flops 9878424576 | bytes 10485760 | tf_op jit(solution)/shard_map/dw_phase/pallas_call | solution.py:337
  372.2 92.2 %ln_backward.1 = bf16[49,512,1024]{2,1,0:T(8,128)(2,1)} custom-call(bf16[49,512,1024]{2,1,0:T(8,128)(2,1)} %bitcast.105, f32[512,1024]{1,0:T(8,128)} %own_dpool.1.da_ref, f32[512,1024]{1,0:T(8,128)} %copy-done.1, f32[1,1024]{1,0:T(1,128)} %bitcast.108, f32[512,128]{1,0:T(8,128)} %get-tuple-element.31.mean_ref, f32[512,128]{1,0:T(8,128)} %get-tuple-element.32.inv_ref), custom_call_target="tpu_custom_call" | custom-call | flops 44820000768 | bytes 102760448 | tf_op jit(solution)/shard_map/ln_backward/pallas_call | solution.py:116
  465.3 1.1 collective-permute-done.14
  467.2 11.0 %place.1 = f32[1024,11264]{1,0:T(8,128)} custom-call(s32[3]{0:T(128)} %pad_add_fusion.sc_ref, f32[1024,11264]{1,0:T(8,128)} %get-tuple-element.42.full_in, f32[1024,1536]{1,0:T(8,128)} %collective-permute-done.12.refs_0_, f32[1024,1024]{1,0:T(8,128)} %collective-permute-done.13.refs_1_), custom_call_target="tpu_custom_call", output_to_operand_aliasing={{}: (1, {})} | custom-call | flops 5976000000 | bytes 20971520 | tf_op jit(solution)/shard_map/place/pallas_call | solution.py:374
  (97 shorter events, 11.2 us)
Async XLA Ops:
  0.6 45.3 %copy-start.6 = (s32[512]{0:T(512)S(1)}, s32[512]{0:T(512)}, u32[]{:S(2)}) copy-start(s32[512]{0:T(512)} %param.15) | copy-start | bytes 6148
  41.1 78.5 %collective-permute-start.9 = (f32[512,1024]{1,0:T(8,128)}, f32[512,1024]{1,0:T(8,128)}, u32[]{:S(2)}, u32[]{:S(2)}) collective-permute-start(f32[512,1024]{1,0:T(8,128)} %get-tuple-element.28.p_ref.refs_0_), channel_id=1, source_target_pairs={{0,1},{1,0},{2,3},{3,2},{4,5},{5,4},{6,7},{7,6},{8,9},{9,8},{10,11... | collective-permute-start | bytes 6291464 | tf_op jit(solution)/shard_map/ppermute | solution.py:398
  41.9 70.6 %collective-permute-start.1 = (f32[512,1024]{1,0:T(8,128)}, f32[512,1024]{1,0:T(8,128)}, u32[]{:S(2)}, u32[]{:S(2)}) collective-permute-start(f32[512,1024]{1,0:T(8,128)} %get-tuple-element.28.p_ref.refs_0_), channel_id=1, source_target_pairs={{0,2},{1,3},{2,0},{3,1},{4,6},{5,7},{6,4},{7,5},{8,10},{9,11},{10,... | collective-permute-start | bytes 6291464 | tf_op jit(solution)/shard_map/ppermute | solution.py:398
  44.4 70.8 %collective-permute-start.3 = (f32[512,1024]{1,0:T(8,128)}, f32[512,1024]{1,0:T(8,128)}, u32[]{:S(2)}, u32[]{:S(2)}) collective-permute-start(f32[512,1024]{1,0:T(8,128)} %get-tuple-element.28.p_ref.refs_0_), channel_id=1, source_target_pairs={{0,4},{1,5},{2,6},{3,7},{4,0},{5,1},{6,2},{7,3},{8,12},{9,13},{10,... | collective-permute-start | bytes 6291464 | tf_op jit(solution)/shard_map/ppermute | solution.py:398
  46.8 53.7 %copy-start.7 = (s32[2]{0:T(128)S(1)}, s32[2]{0:T(128)}, u32[]{:S(2)}) copy-start(s32[2]{0:T(128)} %constant.62.clone) | copy-start | bytes 28
  46.8 56.8 %copy-start.8 = (s32[4]{0:T(128)S(1)}, s32[4]{0:T(128)}, u32[]{:S(2)}) copy-start(s32[4]{0:T(128)} %constant.63.clone) | copy-start | bytes 52
  114.8 39.9 %collective-permute-start.5 = (f32[256,1024]{1,0:T(8,128)}, f32[256,1024]{1,0:T(8,128)}, u32[]{:S(2)}, u32[]{:S(2)}) collective-permute-start(f32[256,1024]{1,0:T(8,128)} %slice.64), channel_id=1, source_target_pairs={{0,4},{1,5},{2,6},{3,7},{4,0},{5,1},{6,2},{7,3},{8,12},{9,13},{10,... | collective-permute-start | bytes 3145736 | tf_op jit(solution)/shard_map/ppermute | solution.py:398
  117.6 37.2 %collective-permute-start.6 = (f32[256,1024]{1,0:T(8,128)}, f32[256,1024]{1,0:T(8,128)}, u32[]{:S(2)}, u32[]{:S(2)}) collective-permute-start(f32[256,1024]{1,0:T(8,128)} %slice.65), channel_id=1, source_target_pairs={{0,2},{1,3},{2,0},{3,1},{4,6},{5,7},{6,4},{7,5},{8,10},{9,11},{10,... | collective-permute-start | bytes 3145736 | tf_op jit(solution)/shard_map/ppermute | solution.py:398
  119.1 71.6 %collective-permute-start.2 = (f32[512,1024]{1,0:T(8,128)}, f32[512,1024]{1,0:T(8,128)}, u32[]{:S(2)}, u32[]{:S(2)}) collective-permute-start(f32[512,1024]{1,0:T(8,128)} %collective-permute-done.1.refs_0_), channel_id=1, source_target_pairs={{0,1},{1,0},{2,3},{3,2},{4,5},{5,4},{6,7},{7,6},{8,9},{9,8},{10,11... | collective-permute-start | bytes 6291464 | tf_op jit(solution)/shard_map/ppermute | solution.py:398
  119.1 71.7 %collective-permute-start.4 = (f32[512,1024]{1,0:T(8,128)}, f32[512,1024]{1,0:T(8,128)}, u32[]{:S(2)}, u32[]{:S(2)}) collective-permute-start(f32[512,1024]{1,0:T(8,128)} %collective-permute-done.3.refs_1_), channel_id=1, source_target_pairs={{0,1},{1,0},{2,3},{3,2},{4,5},{5,4},{6,7},{7,6},{8,9},{9,8},{10,11... | collective-permute-start | bytes 6291464 | tf_op jit(solution)/shard_map/ppermute | solution.py:398
  154.7 36.0 %collective-permute-start.7 = (f32[256,1024]{1,0:T(8,128)}, f32[256,1024]{1,0:T(8,128)}, u32[]{:S(2)}, u32[]{:S(2)}) collective-permute-start(f32[256,1024]{1,0:T(8,128)} %collective-permute-done.5.refs_2_), channel_id=1, source_target_pairs={{0,1},{1,0},{2,3},{3,2},{4,5},{5,4},{6,7},{7,6},{8,9},{9,8},{10,11... | collective-permute-start | bytes 3145736 | tf_op jit(solution)/shard_map/ppermute | solution.py:398
  154.8 36.0 %collective-permute-start.8 = (f32[256,1024]{1,0:T(8,128)}, f32[256,1024]{1,0:T(8,128)}, u32[]{:S(2)}, u32[]{:S(2)}) collective-permute-start(f32[256,1024]{1,0:T(8,128)} %collective-permute-done.6.refs_3_), channel_id=1, source_target_pairs={{0,1},{1,0},{2,3},{3,2},{4,5},{5,4},{6,7},{7,6},{8,9},{9,8},{10,11... | collective-permute-start | bytes 3145736 | tf_op jit(solution)/shard_map/ppermute | solution.py:398
  214.2 106.0 %collective-permute-start.10 = (f32[1024,1536]{1,0:T(8,128)}, f32[1024,1536]{1,0:T(8,128)}, u32[]{:S(2)}, u32[]{:S(2)}) collective-permute-start(f32[1024,1536]{1,0:T(8,128)} %get-tuple-element.39), channel_id=1, source_target_pairs={{0,1},{1,0},{2,3},{3,2},{4,5},{5,4},{6,7},{7,6},{8,9},{9,8},{10,11... | collective-permute-start | bytes 18874376 | tf_op jit(solution)/shard_map/ppermute | solution.py:398
  238.0 110.4 %collective-permute-start.11 = (f32[1024,1536]{1,0:T(8,128)}, f32[1024,1536]{1,0:T(8,128)}, u32[]{:S(2)}, u32[]{:S(2)}) collective-permute-start(f32[1024,1536]{1,0:T(8,128)} %get-tuple-element.41), channel_id=1, source_target_pairs={{0,1},{1,0},{2,3},{3,2},{4,5},{5,4},{6,7},{7,6},{8,9},{9,8},{10,11... | collective-permute-start | bytes 18874376 | tf_op jit(solution)/shard_map/ppermute | solution.py:398
  239.4 72.4 %copy-start = (f32[512,1024]{1,0:T(8,128)S(1)}, f32[512,1024]{1,0:T(8,128)}, u32[]{:S(2)}) copy-start(f32[512,1024]{1,0:T(8,128)} %get-tuple-element.49) | copy-start | bytes 6291460
  264.0 47.8 %collective-permute-start = (f32[512,1024]{1,0:T(8,128)}, f32[512,1024]{1,0:T(8,128)S(1)}, u32[]{:S(2)}, u32[]{:S(2)}) collective-permute-start(f32[512,1024]{1,0:T(8,128)} %own_dpool.1.da_ref), channel_id=1, source_target_pairs={{0,8},{8,0},{1,9},{9,1},{2,10},{10,2},{3,11},{11,3},{4,12},{12,4},... | collective-permute-start | bytes 6291464 | tf_op jit(solution)/shard_map/ppermute | solution.py:434
  311.7 3.0 copy-start.1
  314.7 1.2 collective-permute-start.15
  316.0 3.7 collective-permute-start.16
  319.7 144.7 %collective-permute-start.17 = (f32[2,1024]{1,0:T(2,128)S(1)}, f32[2,1024]{1,0:T(2,128)S(1)}, u32[]{:S(2)}, u32[]{:S(2)}) collective-permute-start(f32[2,1024]{1,0:T(2,128)S(1)} %fusion.6), channel_id=1, source_target_pairs={{0,4},{1,5},{2,6},{3,7},{4,0},{5,1},{6,2},{7,3},{8,12},{9,13},{10,... | collective-permute-start | bytes 24584 | tf_op jit(solution)/shard_map/ppermute | solution.py:398
  371.7 95.5 %collective-permute-start.13 = (f32[1024,1024]{1,0:T(8,128)}, f32[1024,1024]{1,0:T(8,128)}, u32[]{:S(2)}, u32[]{:S(2)}) collective-permute-start(f32[1024,1024]{1,0:T(8,128)} %get-tuple-element.44), channel_id=1, source_target_pairs={{0,1},{1,0},{2,3},{3,2},{4,5},{5,4},{6,7},{7,6},{8,9},{9,8},{10,11... | collective-permute-start | bytes 12582920 | tf_op jit(solution)/shard_map/ppermute | solution.py:398
  371.7 95.4 %collective-permute-start.12 = (f32[1024,1536]{1,0:T(8,128)}, f32[1024,1536]{1,0:T(8,128)}, u32[]{:S(2)}, u32[]{:S(2)}) collective-permute-start(f32[1024,1536]{1,0:T(8,128)} %get-tuple-element.43), channel_id=1, source_target_pairs={{0,1},{1,0},{2,3},{3,2},{4,5},{5,4},{6,7},{7,6},{8,9},{9,8},{10,11... | collective-permute-start | bytes 18874376 | tf_op jit(solution)/shard_map/ppermute | solution.py:398
  372.2 92.8 %copy-start.4 = (f32[1,1536]{1,0:T(1,128)S(1)}, f32[1,1536]{1,0:T(1,128)}, u32[]{:S(2)}) copy-start(f32[1,1536]{1,0:T(1,128)} %get-tuple-element.46) | copy-start | bytes 18436
  372.2 92.8 %copy-start.3 = (f32[1,1536]{1,0:T(1,128)S(1)}, f32[1,1536]{1,0:T(1,128)}, u32[]{:S(2)}) copy-start(f32[1,1536]{1,0:T(1,128)} %get-tuple-element.45) | copy-start | bytes 18436
  372.2 92.9 %copy-start.5 = (f32[1,1536]{1,0:T(1,128)S(1)}, f32[1,1536]{1,0:T(1,128)}, u32[]{:S(2)}) copy-start(f32[1,1536]{1,0:T(1,128)} %get-tuple-element.47) | copy-start | bytes 18436
  372.2 92.9 %copy-start.2 = (f32[1,1024]{1,0:T(1,128)S(1)}, f32[1,1024]{1,0:T(1,128)}, u32[]{:S(2)}) copy-start(f32[1,1024]{1,0:T(1,128)} %get-tuple-element.48) | copy-start | bytes 12292
  465.2 1.2 collective-permute-start.14

commit v2 on v1

v2 whole, which is shorter than its diff:
```python
import functools

import jax
import jax.numpy as jnp
from jax import lax
from jax.experimental import pallas as pl
from jax.experimental.pallas import tpu as pltpu
from jax.sharding import PartitionSpec as P


VALID = 21841
LN_EPS = 1e-5
SMOOTH = 0.1
F32 = jnp.float32
BF16 = jnp.bfloat16
MIB = 2**20


def _cost(flops, nbytes):
    return pl.CostEstimate(flops=int(flops), bytes_accessed=int(nbytes), transcendentals=0)


def _ln_kernel(f_ref, g_ref, b_ref, p_ref, xm_ref, mean_ref, inv_ref, *, rows, sub, group):
    lane = lax.broadcasted_iota(jnp.int32, (sub, 128), 1)
    tokens, _, width = f_ref.shape
    ones = jnp.ones((width, 128), BF16)

    def step(s, carry):
        r = pl.ds(pl.multiple_of(s * sub, sub), sub)
        acc = jnp.zeros((sub, width), F32)
        means = jnp.zeros((sub, 128), F32)
        invs = jnp.zeros((sub, 128), F32)
        for t0 in range(0, tokens, group):
            xb = f_ref[t0 : t0 + group, r, :].reshape(group * sub, width)
            mu_all = jnp.dot(xb, ones, preferred_element_type=F32) * (1.0 / width)
            mus, ivs = [], []
            for j in range(group):
                mu = mu_all[j * sub : (j + 1) * sub, :]
                x = f_ref[t0 + j, r, :].astype(F32)
                q = jnp.zeros((sub, 128), F32)
                for k in range(width // 128):
                    d = x[:, k * 128 : (k + 1) * 128] - mu
                    q = q + d * d
                var = jnp.sum(q, -1, keepdims=True) * (1.0 / width)
                mus.append(mu)
                ivs.append(lax.rsqrt(var + LN_EPS))
            for j in range(group):
                x = f_ref[t0 + j, r, :].astype(F32)
                hats = [(x[:, k * 128 : (k + 1) * 128] - mus[j]) * ivs[j] for k in range(width // 128)]
                acc = acc + jnp.concatenate(hats, 1)
                hit = lane == t0 + j
                means = jnp.where(hit, mus[j], means)
                invs = jnp.where(hit, ivs[j], invs)
        xm = acc * (1.0 / tokens)
        xm_ref[r, :] = xm
        p_ref[r, :] = (xm * g_ref[...] + b_ref[...]).astype(BF16).astype(F32)
        mean_ref[r, :] = means
        inv_ref[r, :] = invs
        return carry

    lax.fori_loop(0, rows // sub, step, 0)


def _ln_forward(ft, gamma, beta, rows=32, sub=32, group=7):
    tokens, images, width = ft.shape
    return pl.pallas_call(
        functools.partial(_ln_kernel, rows=rows, sub=sub, group=group),
        grid=(images // rows,),
        in_specs=[
            pl.BlockSpec((tokens, rows, width), lambda i: (0, i, 0)),
            pl.BlockSpec((1, width), lambda i: (0, 0)),
            pl.BlockSpec((1, width), lambda i: (0, 0)),
        ],
        out_specs=[pl.BlockSpec((rows, width), lambda i: (i, 0))] * 2 + [pl.BlockSpec((rows, 128), lambda i: (i, 0))] * 2,
        out_shape=[jax.ShapeDtypeStruct((images, width), F32)] * 2 + [jax.ShapeDtypeStruct((images, 128), F32)] * 2,
        compiler_params=pltpu.CompilerParams(vmem_limit_bytes=60 * MIB),
        cost_estimate=_cost(36e-6 * 996e12, tokens * images * width * 2),
        name="ln_forward",
    )(ft, gamma, beta)


def _df_kernel(f_ref, da_ref, db_ref, g_ref, mean_ref, inv_ref, o_ref, mu_all, iv_all, *, rows, sub, group):
    tokens, _, width = f_ref.shape
    lanes = [slice(k * 128, (k + 1) * 128) for k in range(width // 128)]

    def step(s, carry):
        r = pl.ds(pl.multiple_of(s * sub, sub), sub)
        up = (da_ref[r, :] + db_ref[r, :]) * g_ref[...] * (1.0 / tokens)
        up = up - jnp.mean(up, -1, keepdims=True)
        means = mean_ref[r, :]
        invs = inv_ref[r, :]
        for t in range(tokens):
            mu_all[t] = jnp.broadcast_to(means[:, t : t + 1], (sub, 128))
            iv_all[t] = jnp.broadcast_to(invs[:, t : t + 1], (sub, 128))
        for t0 in range(0, tokens, group):
            scales = []
            for t in range(t0, t0 + group):
                x = f_ref[t, r, :].astype(F32)
                mu, iv = mu_all[t], iv_all[t]
                q = jnp.zeros((sub, 128), F32)
                for c in lanes:
                    q = q + (x[:, c] - mu) * up[:, c]
                proj = jnp.sum(q, -1, keepdims=True) * (1.0 / width)
                scales.append(proj * iv * iv * iv)
            for t in range(t0, t0 + group):
                x = f_ref[t, r, :].astype(F32)
                mu, iv, k = mu_all[t], iv_all[t], scales[t - t0]
                o_ref[t, r, :] = jnp.concatenate([iv * up[:, c] - (x[:, c] - mu) * k for c in lanes], 1).astype(BF16)
        return carry

    lax.fori_loop(0, rows // sub, step, 0)


def _ln_backward(ft, dpool_a, dpool_b, gamma, means, invs, rows=64, sub=32, group=7):
    tokens, images, width = ft.shape
    row_block = pl.BlockSpec((rows, width), lambda i: (i, 0))
    stat_block = pl.BlockSpec((rows, 128), lambda i: (i, 0))
    return pl.pallas_call(
        functools.partial(_df_kernel, rows=rows, sub=sub, group=group),
        grid=(images // rows,),
        in_specs=[
            pl.BlockSpec((tokens, rows, width), lambda i: (0, i, 0)),
            row_block,
            row_block,
            pl.BlockSpec((1, width), lambda i: (0, 0)),
            stat_block,
            stat_block,
        ],
        out_specs=pl.BlockSpec((tokens, rows, width), lambda i: (0, i, 0)),
        out_shape=jax.ShapeDtypeStruct((tokens, images, width), BF16),
        scratch_shapes=[pltpu.VMEM((tokens, sub, 128), F32)] * 2,
        compiler_params=pltpu.CompilerParams(vmem_limit_bytes=60 * MIB),
        cost_estimate=_cost(45e-6 * 996e12, tokens * images * width * 4),
        name="ln_backward",
    )(ft, dpool_a, dpool_b, gamma, means, invs)


def _masked(w, bias, col):
    valid = col < VALID
    return jnp.where(valid, w, jnp.zeros((), BF16)), jnp.where(valid, bias, -1e30)


def _dlogit(logit, shift, col, y, total):
    flat = jnp.where(col < VALID, SMOOTH / VALID / total, 0.0)
    drop = jnp.where(col == y, (SMOOTH / VALID + 1.0 - SMOOTH) / total, flat)
    return jnp.exp(logit - shift) - drop


def _rows_to_columns(rows):
    return jnp.concatenate([rows] * 16, 0).T


def _head_kernel(p_ref, w_ref, b_ref, y_ref, o_ref, sh_ref, l_all, m_acc, s_acc, t_acc, v_acc, p16, mine, other, send, every, shift, zs, zr, ds, dr, *, tile, steps, row_block, total, dp_size):
    i = pl.program_id(0)
    tp_i, dp_i = lax.axis_index("tp"), lax.axis_index("dp")
    images = p16.shape[0]
    t = lax.rem(i, steps)
    col = tp_i * (tile * steps) + t * tile + lax.broadcasted_iota(jnp.int32, (1, tile), 1)
    lane = lax.broadcasted_iota(jnp.int32, (1, 128), 1)
    barrier = pltpu.get_barrier_semaphore()
    mesh_id = pl.DeviceIdType.MESH
    across = pltpu.make_async_remote_copy(mine, other, zs, zr, device_id=(1 - tp_i, dp_i), device_id_type=mesh_id)
    casts = [
        pltpu.make_async_remote_copy(
            send, every.at[dp_i], ds.at[j], dr.at[j], device_id=(tp_i, lax.rem(dp_i + j + 1, dp_size)), device_id_type=mesh_id
        )
        for j in range(dp_size - 1)
    ]

    @pl.when(i == 0)
    def _():
        pl.semaphore_signal(barrier, inc=1, device_id=(1 - tp_i, dp_i), device_id_type=mesh_id)
        for j in range(dp_size - 1):
            pl.semaphore_signal(barrier, inc=1, device_id=(tp_i, lax.rem(dp_i + j + 1, dp_size)), device_id_type=mesh_id)
        m_acc[...] = jnp.full(m_acc.shape, -jnp.inf, F32)
        for acc in (s_acc, t_acc, v_acc):
            acc[...] = jnp.zeros(acc.shape, F32)
        p16[...] = p_ref[...].astype(BF16)

    @pl.when(i < steps)
    def _():
        w, bias = _masked(w_ref[...], b_ref[...], col)
        groups = [slice(k * 128, (k + 1) * 128) for k in range(tile // 128)]
        bsum = jnp.zeros((1, 128), F32)
        kept = jnp.where(col < VALID, b_ref[...], 0.0)
        for g in groups:
            bsum = bsum + kept[:, g]
        for r0 in range(0, images, row_block):
            r = slice(r0, r0 + row_block)
            raw = jnp.dot(p16[r, :], w, preferred_element_type=F32)
            logit = raw + bias
            l_all[t, r, :] = logit
            target = jnp.where(col == y_ref[r, :], logit, 0.0)
            m0 = m_acc[r, :]
            m = m0
            for g in groups:
                m = jnp.maximum(m, logit[:, g])
            s = s_acc[r, :] * jnp.exp(m0 - m)
            tt, v = t_acc[r, :], v_acc[r, :] + bsum
            for g in groups:
                s = s + jnp.exp(logit[:, g] - m)
                tt = tt + target[:, g]
                v = v + raw[:, g]
            m_acc[r, :] = m
            s_acc[r, :] = s
            t_acc[r, :] = tt
            v_acc[r, :] = v

    @pl.when(i == steps - 1)
    def _():
        m = m_acc[...]
        top = jnp.max(m, -1, keepdims=True)
        norm = jnp.sum(s_acc[...] * jnp.exp(m - top), -1, keepdims=True)
        target = jnp.sum(t_acc[...], -1, keepdims=True)
        valid_sum = jnp.sum(v_acc[...], -1, keepdims=True)
        stats = jnp.where(lane == 0, top, jnp.where(lane == 1, norm, jnp.where(lane == 2, target, valid_sum)))
        mine[...] = stats.T[:8, :]

    @pl.when(i == steps)
    def _():
        pl.semaphore_wait(barrier, dp_size)
        across.start()
        across.wait()
        a, b = mine[...], other[...]
        top = jnp.maximum(a[0:1], b[0:1])
        lse = top + jnp.log(a[1:2] * jnp.exp(a[0:1] - top) + b[1:2] * jnp.exp(b[0:1] - top))
        loss = lse - (1.0 - SMOOTH) * (a[2:3] + b[2:3]) - (SMOOTH / VALID) * (a[3:4] + b[3:4])
        row = lax.broadcasted_iota(jnp.int32, (8, images), 0)
        rows = jnp.where(row == 0, lse + jnp.log(F32(total)), jnp.where(row == 1, loss, 0.0))
        cols = _rows_to_columns(rows)
        shift[...] = cols
        out = jnp.where(lane == 2, y_ref[...].astype(F32), cols)
        send[...] = out.T[:8, :]

    @pl.when(i == steps + 1)
    def _():
        every[dp_i] = send[...]
        for c in casts:
            c.start()

    @pl.when(i >= steps)
    def _():
        for r0 in range(0, images, row_block):
            r = slice(r0, r0 + row_block)
            d = _dlogit(l_all[t, r, :], shift[r, 0:1], col, y_ref[r, :], total).astype(BF16)
            part = lax.dot_general(d, w_ref[...], (((1,), (1,)), ((), ())), preferred_element_type=F32)
            o_ref[r, :] = jnp.where(i == steps, part, o_ref[r, :] + part)

    @pl.when(i == 2 * steps - 1)
    def _():
        for c in casts:
            c.wait()
        sh_ref[...] = every[...]


def _own_head(p, w, b, y, dp_size, tile=1024, row_block=256):
    images, width = p.shape
    cols = w.shape[1]
    steps = cols // tile
    dma = pltpu.SemaphoreType.DMA
    small = pltpu.VMEM((8, images), F32)
    return pl.pallas_call(
        functools.partial(_head_kernel, tile=tile, steps=steps, row_block=row_block, total=images * dp_size, dp_size=dp_size),
        grid=(2 * steps,),
        in_specs=[
            pl.BlockSpec((images, width), lambda i: (0, 0)),
            pl.BlockSpec((width, tile), lambda i: (0, lax.rem(i, steps))),
            pl.BlockSpec((1, tile), lambda i: (0, lax.rem(i, steps))),
            pl.BlockSpec((images, 1), lambda i: (0, 0)),
        ],
        out_specs=[pl.BlockSpec((images, width), lambda i: (0, 0)), pl.BlockSpec((dp_size, 8, images), lambda i: (0, 0, 0))],
        out_shape=[jax.ShapeDtypeStruct((images, width), F32), jax.ShapeDtypeStruct((dp_size, 8, images), F32)],
        scratch_shapes=[pltpu.VMEM((steps, images, tile), F32)]
        + [pltpu.VMEM((images, 128), F32)] * 4
        + [pltpu.VMEM((images, width), BF16), small, small, small, pltpu.VMEM((dp_size, 8, images), F32), pltpu.VMEM((images, 128), F32)]
        + [dma, dma, dma((dp_size - 1,)), dma((dp_size - 1,))],
        compiler_params=pltpu.CompilerParams(vmem_limit_bytes=60 * MIB, collective_id=0, has_side_effects=True),
        cost_estimate=_cost(4 * images * width * cols, width * cols * 4),
        name="own_head",
    )(p, w, b, y)


def _dw_kernel(sc_ref, *refs, counts, sets, tile, row_block, total, has_acc, to_full, aliased, give_p, plan, off):
    refs = list(refs)
    take = lambda n: [refs.pop(0) for _ in range(n)]
    p_refs = take(len(counts))
    sh_refs = take(sets)
    w_ref, b_ref = take(2)
    acc_ref, acc_db_ref = take(2) if has_acc else (None, None)
    got_ref = None
    if aliased:
        take(1)
        if aliased > 1:
            (got_ref,) = take(1)
    (full_ref,) = take(1) if to_full else (None,)
    o_ref, db_ref = take(2)
    (give_ref,) = take(1) if give_p else (None,)
    p16, d16, stat = refs[-3:] if p_refs[0].dtype != BF16 else (p_refs[0], *refs[-2:])
    images = d16.shape[0]
    i = pl.program_id(0)

    @pl.when(i == 0)
    def _():
        if p16 is not p_refs[0]:
            r0 = 0
            for ref, n in zip(p_refs, counts):
                p16[r0 : r0 + n, :] = ref[...].astype(BF16)
                r0 += n
            if give_p:
                give_ref[...] = p16[...]
        n = images // sets
        for k, ref in enumerate(sh_refs):
            stat[k * n : (k + 1) * n, :] = _rows_to_columns(ref[0])

    def compute():
        col = sc_ref[0] + (off + plan.own(i)) * tile + lax.broadcasted_iota(jnp.int32, (1, tile), 1)
        w, bias = _masked(w_ref[...], b_ref[...], col)
        db = jnp.zeros((1, tile), F32)
        for r0 in range(0, images, row_block):
            r = slice(r0, r0 + row_block)
            logit = jnp.dot(p16[r, :], w, preferred_element_type=F32) + bias
            d = _dlogit(logit, stat[r, 0:1], col, stat[r, 2:3].astype(jnp.int32), total)
            db = db + jnp.sum(d, 0, keepdims=True)
            d16[r, :] = d.astype(BF16)
        out = lax.dot_general(p16[...], d16[...], (((0,), (0,)), ((), ())), preferred_element_type=F32)
        if has_acc:
            out = out + acc_ref[...]
            db = db + acc_db_ref[...]
        o_ref[...] = out
        if to_full:
            full_ref[...] = out
        db_ref[...] = db

    if got_ref is None:
        compute()
    else:
        pl.when(plan.is_own(i))(compute)

        @pl.when(jnp.logical_not(plan.is_own(i)))
        def _():
            full_ref[...] = got_ref[...]


class _Plan:
    def __init__(self, own, extra):
        self.n, self.e, self.m = own, extra, min(own, extra)

    def is_own(self, i):
        tail = i >= 2 * self.m
        return jnp.where(tail, self.n > self.e, lax.rem(i, 2) == 0)

    def own(self, i):
        return jnp.minimum(jnp.where(i < 2 * self.m, (i + 1) // 2, i - self.m), self.n - 1)

    def last(self, i):
        return jnp.minimum(jnp.where(i < 2 * self.m, i // 2, i - self.m), self.n - 1)

    def copy(self, i):
        return jnp.clip(jnp.where(i < 2 * self.m, i // 2, i - self.m), 0, max(self.e - 1, 0))


def _dw_phase(sc, pooled, slots, shifts, w, b, total, acc=None, own=None, off=0, full=None, got=None, got_off=0, to_full=False, give_p=False, tile=512, row_block=512):
    counts = [p.shape[0] for p in pooled]
    images = sum(counts)
    width, cols = w.shape
    own = own or cols // 2 // tile
    plan = _Plan(own, got.shape[1] // tile if got is not None else 0)
    in_specs = [pl.BlockSpec(p.shape, lambda i, s: (0, 0)) for p in pooled]
    in_specs += [pl.BlockSpec((1, *shifts.shape[1:]), lambda i, s, k=k: (s[3 + k], 0, 0)) for k in slots]
    in_specs += [
        pl.BlockSpec((width, tile), lambda i, s: (0, s[1] + off + plan.own(i))),
        pl.BlockSpec((1, tile), lambda i, s: (0, s[1] + off + plan.own(i))),
    ]
    args = list(pooled) + [shifts] * len(slots) + [w, b]
    if acc is not None:
        in_specs += [pl.BlockSpec((width, tile), lambda i, s: (0, off + plan.own(i))), pl.BlockSpec((1, tile), lambda i, s: (0, off + plan.own(i)))]
        args += list(acc)
    aliases = {}
    aliased = 0
    if full is not None:
        aliased = 1
        aliases = {len(args) + 1: 0}
        in_specs.append(pl.BlockSpec(memory_space=pl.ANY))
        args.append(full)
    if got is not None:
        aliased = 2
        in_specs.append(pl.BlockSpec((width, tile), lambda i, s: (0, plan.copy(i))))
        args.append(got)
    out_specs = [pl.BlockSpec((width, tile), lambda i, s: (0, plan.last(i))), pl.BlockSpec((1, tile), lambda i, s: (0, plan.last(i)))]
    out_shape = [jax.ShapeDtypeStruct((width, own * tile), F32), jax.ShapeDtypeStruct((1, own * tile), F32)]
    if to_full:
        place = lambda i, s: (0, jnp.where(plan.is_own(i), s[1] + off + plan.last(i), s[2] + got_off + plan.copy(i)))
        out_specs.insert(0, pl.BlockSpec((width, tile), place))
        out_shape.insert(0, jax.ShapeDtypeStruct((width, cols), F32))
    if give_p:
        out_specs.append(pl.BlockSpec((images, width), lambda i, s: (0, 0)))
        out_shape.append(jax.ShapeDtypeStruct((images, width), BF16))
    scratch = [pltpu.VMEM((images, tile), BF16), pltpu.VMEM((images, 128), F32)]
    if pooled[0].dtype != BF16:
        scratch.insert(0, pltpu.VMEM((images, width), BF16))
    return pl.pallas_call(
        functools.partial(
            _dw_kernel,
            counts=counts,
            sets=len(slots),
            tile=tile,
            row_block=row_block,
            total=total,
            has_acc=acc is not None,
            to_full=to_full,
            aliased=aliased,
            give_p=give_p,
            plan=plan,
            off=off,
        ),
        grid_spec=pltpu.PrefetchScalarGridSpec(
            num_scalar_prefetch=1, grid=(plan.n + plan.e,), in_specs=in_specs, out_specs=out_specs, scratch_shapes=scratch
        ),
        out_shape=out_shape,
        input_output_aliases=aliases,
        compiler_params=pltpu.CompilerParams(vmem_limit_bytes=63 * MIB),
        cost_estimate=_cost(4.6 * images * width * own * tile, width * own * tile * 10),
        name="dw_phase",
    )(sc, *args)


def _place_kernel(sc_ref, full_in, *refs, starts):
    parts, full_ref = refs[:-1], refs[-1]
    i = pl.program_id(0)
    for ref, start, stop in zip(parts, starts[:-1], starts[1:]):

        @pl.when((i >= start) & (i < stop))
        def _():
            full_ref[...] = ref[...]


def _place(sc, full, parts, off, tile=512):
    width, cols = full.shape
    starts = [0]
    for part in parts:
        starts.append(starts[-1] + part.shape[1] // tile)
    specs = [
        pl.BlockSpec((width, tile), lambda i, s, lo=lo, hi=hi: (0, jnp.clip(i - lo, 0, hi - lo - 1))) for lo, hi in zip(starts[:-1], starts[1:])
    ]
    return pl.pallas_call(
        functools.partial(_place_kernel, starts=starts),
        grid_spec=pltpu.PrefetchScalarGridSpec(
            num_scalar_prefetch=1,
            grid=(starts[-1],),
            in_specs=[pl.BlockSpec(memory_space=pl.ANY)] + specs,
            out_specs=pl.BlockSpec((width, tile), lambda i, s: (0, s[2] + off + i)),
        ),
        out_shape=jax.ShapeDtypeStruct((width, cols), F32),
        input_output_aliases={1: 0},
        compiler_params=pltpu.CompilerParams(vmem_limit_bytes=60 * MIB),
        cost_estimate=_cost(6e-6 * 996e12, width * starts[-1] * tile * 8),
        name="place",
    )(sc, full, *parts)


CHUNKS = (3, 3, 3, 2)
TILE = 512


def solution(mesh):
    dp_size, tp_size = mesh.shape["dp"], mesh.shape["tp"]

    def swap(x, bit):
        return lax.ppermute(x, "dp", [(i, i ^ bit) for i in range(dp_size)])

    def head(feats, ln_gamma, ln_beta, w, b, labels):
        images, _, width = feats.shape
        cols = w.shape[1]
        total = images * dp_size
        tp_i, dp_i = lax.axis_index("tp"), lax.axis_index("dp")
        core = dp_i % 2
        half_tiles = cols // 2 // TILE
        bits = (0, 1, 2, 4, 3, 5, 6, 7)
        sc = jnp.stack([tp_i * cols + core * (cols // 2), core * half_tiles, (1 - core) * half_tiles] + [dp_i ^ k for k in bits]).astype(jnp.int32)
        ft = jnp.transpose(feats, (1, 0, 2))
        gamma, beta, bias = ln_gamma.reshape(1, width), ln_beta.reshape(1, width), b.reshape(1, cols)

        p, xm, means, invs = _ln_forward(ft, gamma, beta)
        p_core, p_x, p_y = swap(p, 1), swap(p, 2), swap(p, 4)

        dpool_a, shifts = _own_head(p, w, bias, labels.reshape(images, 1), dp_size)
        dpool_b = lax.ppermute(dpool_a, "tp", [(i, tp_size - 1 - i) for i in range(tp_size)])

        acc = _dw_phase(sc, [p, p_core], (0, 1), shifts, w, bias, total)
        acc = _dw_phase(sc, [p_x, p_y], (2, 3), shifts, w, bias, total, acc=acc)
        half = images // 2
        p_d = [swap(p_x[:half], 4), swap(p_y[half:], 2)]
        p_rest = [swap(p_x, 1), swap(p_y, 1)] + p_d
        p_rest += [swap(p_d[0], 1), swap(p_d[1], 1)]

        full, sent, dbs, offs, off = None, [], [], [], 0
        for c, n in enumerate(CHUNKS):
            got = sent[c - 2] if c >= 2 else None
            full, part, db, *rest = _dw_phase(
                sc,
                p_rest,
                (4, 5, 6, 7),
                shifts,
                w,
                bias,
                total,
                acc=acc,
                own=n,
                off=off,
                full=full,
                got=got,
                got_off=offs[c - 2] if c >= 2 else 0,
                to_full=True,
                give_p=c == 0,
            )
            p_rest = rest or p_rest
            sent.append(swap(part, 1))
            dbs.append(db)
            offs.append(off)
            off += n

        db_mine = jnp.concatenate(dbs, 1)
        db_other = swap(db_mine, 1)
        grad_b = jnp.where(core == 0, jnp.concatenate([db_mine, db_other], 1), jnp.concatenate([db_other, db_mine], 1)).reshape(cols)

        dpool = dpool_a + dpool_b
        loss_own = jnp.sum(lax.dynamic_index_in_dim(shifts, dp_i, 0, keepdims=False)[1])
        sums = jnp.stack([jnp.sum(dpool * xm, 0), jnp.sum(dpool, 0), jnp.broadcast_to(loss_own / total, (width,))])
        for bit in (1, 2, 4):
            sums = sums + swap(sums, bit)

        dft = _ln_backward(ft, dpool_a, dpool_b, gamma, means, invs)
        full = _place(sc, full, sent[-2:], offs[-2])
        return sums[2, 0], jnp.transpose(dft, (1, 0, 2)), full, grad_b, sums[0], sums[1]

    return jax.shard_map(
        head,
        mesh=mesh,
        in_specs=(P("dp", None, None), P(), P(), P(None, "tp"), P("tp"), P("dp")),
        out_specs=(P(), P("dp", None, None), P(None, "tp"), P("tp"), P(), P()),
        check_vma=False,
    )
```

time: 486 us -> 387 us (0.80); the launches traced: 480 us -> 386 us
  Pallas kernels: 364 us -> 309 us
  blocking collectives: 25.4 us -> 0 us
  local copies, waits for them, and re-layouts: 18.6 us -> 8.75 us
    pallas_call x1, Pallas kernels: 92.2 us -> 44.6 us  [_ln_backward(): pl.pallas_call(functools.partial(_df_kernel, rows=rows, sub=sub, group=gr...]
    all_gather x1 -> x0, blocking collectives: 25.4 us -> none  [head(): every = lax.all_gather(rows, ('tp', 'dp'))]
    pallas_call x8 -> x7, Pallas kernels: 221 us -> 212 us  [the longest x6 165 us: _dw_phase(): pl.pallas_call(functools.partial(_dw_kernel, counts=counts, sets=len(slot...]
    unnamed x38 -> x20, local copies, waits for them, and re-layouts: 7.05 us -> 1.39 us
  transfers between devices with their start and end apart: 18 -> 18, of which waited for: 4 -> 4; matrix products, arithmetic and copies ran while one was open for 5% -> 3% of each run, Pallas kernels for 60% -> 61%
where the time goes in v2:
time: 387 us; the launch traced here: 386 us
  Pallas kernels  309 us (80%)
  waiting for transfers between devices  48.8 us (13%)
  starting transfers between devices  13.3 us (3%)
  local copies, waits for them, and re-layouts  8.75 us (2%)
  other arithmetic  5.2 us (1%)
    pallas_call x6, Pallas kernels, _dw_phase(): pl.pallas_call(functools.partial(_dw_kernel, counts=counts, sets=len(slot...  165 us
    pallas_call x1, Pallas kernels, _own_head(): pl.pallas_call(functools.partial(_head_kernel, tile=tile, steps=steps, ro...  47.7 us
    pallas_call x1, Pallas kernels, _ln_backward(): pl.pallas_call(functools.partial(_df_kernel, rows=rows, sub=sub, group=gr...  44.6 us
    ppermute x1, waiting for transfers between devices, head(): lax.ppermute(dpool_a, 'tp', [(i, tp_size - 1 - i) for i in range(tp_size)])  44.2 us
    pallas_call x1, Pallas kernels, _ln_forward(): pl.pallas_call(functools.partial(_ln_kernel, rows=rows, sub=sub, group=gr...  40.5 us
    ppermute x17, starting transfers between devices, swap(): return lax.ppermute(x, 'dp', [(i, i ^ bit) for i in range(dp_size)])  11.8 us
    pallas_call x1, Pallas kernels, _place(): pl.pallas_call(functools.partial(_place_kernel, starts=starts), grid_spec...  11 us
  transfers between devices with their start and end apart: 18, of which 4 were waited for; matrix products, arithmetic and copies ran while one was open for 3% of the time, Pallas kernels for 61%

profile of v2, /device:TPU:0, one launch (start us, length us, event | category | flops | bytes accessed | tf_op | source)
XLA Modules:
  0.0 386.2 jit_solution(15150059041499412837)
XLA Ops:
  0.6 40.5 %ln_forward.1 = (f32[512,1024]{1,0:T(8,128)}, f32[512,1024]{1,0:T(8,128)}, f32[512,128]{1,0:T(8,128)}, f32[512,128]{1,0:T(8,128)}) custom-call(bf16[49,512,1024]{2,1,0:T(8,128)(2,1)} %bitcast.42, f32[1,1024]{1,0:T(1,128)} %bitcast.45, f32[1,1024]{1,0:T(1,128)} %bitcast.44), custom_call_target="tpu_custom_call" | custom-call | flops 35855998976 | bytes 51380224 | tf_op jit(solution)/shard_map/ln_forward/pallas_call | solution.py:66
  41.1 0.7 collective-permute-start.12
  41.8 2.5 collective-permute-start.4
  44.4 1.5 collective-permute-start.6
  45.9 0.9 copy.16.y_ref
  46.8 0.6 stack.59.sc_ref
  47.4 47.7 %own_head.1 = (f32[512,1024]{1,0:T(8,128)}, f32[8,8,512]{2,1,0:T(8,128)}) custom-call(f32[512,1024]{1,0:T(8,128)} %get-tuple-element.29.p_ref.refs_0_, bf16[1024,11264]{1,0:T(8,128)(2,1)} %refs_5_.5, f32[1,11264]{1,0:T(1,128)} %bitcast.24, s32[512,1]{1,0:T(8,128)} %copy.16.y_ref), custom_call_target="tpu_custom_call" | custom-call | flops 23622320128 | bytes 46137344 | tf_op jit(solution)/shard_map/own_head/pallas_call | solution.py:262
  95.1 2.4 slice.26
  97.4 1.5 collective-permute-start.8
  99.0 2.3 slice.27
  101.3 0.5 collective-permute-start.9
  102.3 33.7 %dw_phase.6 = (f32[1024,5632]{1,0:T(8,128)}, f32[1,5632]{1,0:T(1,128)}) custom-call(s32[11]{0:T(128)} %stack.59.sc_ref, f32[512,1024]{1,0:T(8,128)} %get-tuple-element.29.p_ref.refs_0_, f32[512,1024]{1,0:T(8,128)} %collective-permute-done.12.refs_1_, f32[8,8,512]{2,1,0:T(8,128)} %get-tuple-element.32.refs_2_.refs_3_.refs_6_.refs_7_.refs_8_.refs_9_.refs_1_.refs_4_, ...), custom_call_target="tpu_custom_call" | custom-call | flops 27165667328 | bytes 57671680 | tf_op jit(solution)/shard_map/dw_phase/pallas_call | solution.py:401
  136.6 34.7 %dw_phase.7 = (f32[1024,5632]{1,0:T(8,128)}, f32[1,5632]{1,0:T(1,128)}) custom-call(s32[11]{0:T(128)} %stack.59.sc_ref, f32[512,1024]{1,0:T(8,128)} %collective-permute-done.4.refs_0_, f32[512,1024]{1,0:T(8,128)} %collective-permute-done.6.refs_1_, f32[8,8,512]{2,1,0:T(8,128)} %get-tuple-element.32.refs_2_.refs_3_.refs_6_.refs_7_.refs_8_.refs_9_.refs_1_.refs_4_, ...), custom_call_target="tpu_custom_call" | custom-call | flops 27165667328 | bytes 57671680 | tf_op jit(solution)/shard_map/dw_phase/pallas_call | solution.py:401
  171.3 23.2 %dw_phase.8 = (f32[1024,11264]{1,0:T(8,128)}, f32[1024,1536]{1,0:T(8,128)}, f32[1,1536]{1,0:T(1,128)}, bf16[2048,1024]{1,0:T(8,128)(2,1)}) custom-call(s32[11]{0:T(128)} %stack.59.sc_ref, f32[512,1024]{1,0:T(8,128)} %collective-permute-done.5.refs_0_, f32[512,1024]{1,0:T(8,128)} %collective-permute-done.7.refs_1_, ...), custom_call_target="tpu_custom_call" | custom-call | flops 14817637376 | bytes 15728640 | tf_op jit(solution)/shard_map/dw_phase/pallas_call | solution.py:401
  194.6 21.1 %dw_phase.9 = (f32[1024,11264]{1,0:T(8,128)}, f32[1024,1536]{1,0:T(8,128)}, f32[1,1536]{1,0:T(1,128)}) custom-call(s32[11]{0:T(128)} %stack.59.sc_ref, bf16[2048,1024]{1,0:T(8,128)(2,1)} %get-tuple-element.39.refs_0_, f32[8,8,512]{2,1,0:T(8,128)} %get-tuple-element.32.refs_2_.refs_3_.refs_6_.refs_7_.refs_8_.refs_9_.refs_1_.refs_4_, ...), custom_call_target="tpu_custom_call", output_to_operand_aliasing={{0}: (10, {})} | custom-call | flops 14817637376 | bytes 15728640 | tf_op jit(solution)/shard_map/dw_phase/pallas_call | solution.py:401
  216.2 1.6 collective-permute-start
  217.7 1.3 dynamic-slice_reduce_fusion
  219.8 44.2 %collective-permute-done.db_ref = f32[512,1024]{1,0:T(8,128)S(1)} collective-permute-done((f32[512,1024]{1,0:T(8,128)}, f32[512,1024]{1,0:T(8,128)S(1)}, u32[]{:S(2)}, u32[]{:S(2)}) %collective-permute-start) | collective-permute-done | bytes 2097184 | tf_op jit(solution)/shard_map/ppermute | solution.py:487
  264.0 1.3 copy-done
  265.3 2.9 multiply_reduce_fusion
  268.2 1.2 collective-permute-done.1
  269.5 1.5 collective-permute-start.2
  271.0 2.3 collective-permute-done.2
  273.3 1.2 collective-permute-start.3
  274.5 29.0 %dw_phase.10 = (f32[1024,11264]{1,0:T(8,128)}, f32[1024,1536]{1,0:T(8,128)}, f32[1,1536]{1,0:T(1,128)}) custom-call(s32[11]{0:T(128)} %stack.59.sc_ref, bf16[2048,1024]{1,0:T(8,128)(2,1)} %get-tuple-element.39.refs_0_, ...), custom_call_target="tpu_custom_call", output_to_operand_aliasing={{0}: (10, {})} | custom-call | flops 14817637376 | bytes 15728640 | tf_op jit(solution)/shard_map/dw_phase/pallas_call | solution.py:401
  303.5 23.2 %dw_phase.11 = (f32[1024,11264]{1,0:T(8,128)}, f32[1024,1024]{1,0:T(8,128)}, f32[1,1024]{1,0:T(1,128)}) custom-call(s32[11]{0:T(128)} %stack.59.sc_ref, bf16[2048,1024]{1,0:T(8,128)(2,1)} %get-tuple-element.39.refs_0_, ...), custom_call_target="tpu_custom_call", output_to_operand_aliasing={{0}: (10, {})} | custom-call | flops 9878424576 | bytes 10485760 | tf_op jit(solution)/shard_map/dw_phase/pallas_call | solution.py:401
  327.3 44.6 %ln_backward.1 = bf16[49,512,1024]{2,1,0:T(8,128)(2,1)} custom-call(bf16[49,512,1024]{2,1,0:T(8,128)(2,1)} %bitcast.43, f32[512,1024]{1,0:T(8,128)} %get-tuple-element.30.da_ref, f32[512,1024]{1,0:T(8,128)} %copy-done, f32[1,1024]{1,0:T(1,128)} %bitcast.46, f32[512,128]{1,0:T(8,128)} %get-tuple-element.33.mean_ref, f32[512,128]{1,0:T(8,128)} %get-tuple-element.34.inv_ref), custom_call_target="tpu_custom_call" | custom-call | flops 44820000768 | bytes 102760448 | tf_op jit(solution)/shard_map/ln_backward/pallas_call | solution.py:118
  371.9 0.5 slice.25
  372.4 0.6 fusion.1
  373.3 1.1 collective-permute-done.17
  374.6 0.6 broadcast_select_fusion
  375.2 11.0 %place.1 = f32[1024,11264]{1,0:T(8,128)} custom-call(s32[11]{0:T(128)} %stack.59.sc_ref, f32[1024,11264]{1,0:T(8,128)} %get-tuple-element.45.full_in, f32[1024,1536]{1,0:T(8,128)} %collective-permute-done.15.refs_0_, f32[1024,1024]{1,0:T(8,128)} %collective-permute-done.16.refs_1_), custom_call_target="tpu_custom_call", output_to_operand_aliasing={{}: (1, {})} | custom-call | flops 5976000000 | bytes 20971520 | tf_op jit(solution)/shard_map/place/pallas_call | solution.py:445
  (56 shorter events, 2.8 us)
Async XLA Ops:
  0.6 45.3 %copy-start.5 = (s32[512]{0:T(512)S(1)}, s32[512]{0:T(512)}, u32[]{:S(2)}) copy-start(s32[512]{0:T(512)} %param.11) | copy-start | bytes 6148
  41.1 61.2 %collective-permute-start.12 = (f32[512,1024]{1,0:T(8,128)}, f32[512,1024]{1,0:T(8,128)}, u32[]{:S(2)}, u32[]{:S(2)}) collective-permute-start(f32[512,1024]{1,0:T(8,128)} %get-tuple-element.29.p_ref.refs_0_), channel_id=1, source_target_pairs={{0,1},{1,0},{2,3},{3,2},{4,5},{5,4},{6,7},{7,6},{8,9},{9,8},{10,11... | collective-permute-start | bytes 6291464 | tf_op jit(solution)/shard_map/ppermute | solution.py:469
  41.8 53.2 %collective-permute-start.4 = (f32[512,1024]{1,0:T(8,128)}, f32[512,1024]{1,0:T(8,128)}, u32[]{:S(2)}, u32[]{:S(2)}) collective-permute-start(f32[512,1024]{1,0:T(8,128)} %get-tuple-element.29.p_ref.refs_0_), channel_id=1, source_target_pairs={{0,2},{1,3},{2,0},{3,1},{4,6},{5,7},{6,4},{7,5},{8,10},{9,11},{10,... | collective-permute-start | bytes 6291464 | tf_op jit(solution)/shard_map/ppermute | solution.py:469
  44.4 54.6 %collective-permute-start.6 = (f32[512,1024]{1,0:T(8,128)}, f32[512,1024]{1,0:T(8,128)}, u32[]{:S(2)}, u32[]{:S(2)}) collective-permute-start(f32[512,1024]{1,0:T(8,128)} %get-tuple-element.29.p_ref.refs_0_), channel_id=1, source_target_pairs={{0,4},{1,5},{2,6},{3,7},{4,0},{5,1},{6,2},{7,3},{8,12},{9,13},{10,... | collective-permute-start | bytes 6291464 | tf_op jit(solution)/shard_map/ppermute | solution.py:469
  97.4 38.6 %collective-permute-start.8 = (f32[256,1024]{1,0:T(8,128)}, f32[256,1024]{1,0:T(8,128)}, u32[]{:S(2)}, u32[]{:S(2)}) collective-permute-start(f32[256,1024]{1,0:T(8,128)} %slice.26), channel_id=1, source_target_pairs={{0,4},{1,5},{2,6},{3,7},{4,0},{5,1},{6,2},{7,3},{8,12},{9,13},{10,... | collective-permute-start | bytes 3145736 | tf_op jit(solution)/shard_map/ppermute | solution.py:469
  101.3 34.8 %collective-permute-start.9 = (f32[256,1024]{1,0:T(8,128)}, f32[256,1024]{1,0:T(8,128)}, u32[]{:S(2)}, u32[]{:S(2)}) collective-permute-start(f32[256,1024]{1,0:T(8,128)} %slice.27), channel_id=1, source_target_pairs={{0,2},{1,3},{2,0},{3,1},{4,6},{5,7},{6,4},{7,5},{8,10},{9,11},{10,... | collective-permute-start | bytes 3145736 | tf_op jit(solution)/shard_map/ppermute | solution.py:469
  101.8 69.5 %collective-permute-start.5 = (f32[512,1024]{1,0:T(8,128)}, f32[512,1024]{1,0:T(8,128)}, u32[]{:S(2)}, u32[]{:S(2)}) collective-permute-start(f32[512,1024]{1,0:T(8,128)} %collective-permute-done.4.refs_0_), channel_id=1, source_target_pairs={{0,1},{1,0},{2,3},{3,2},{4,5},{5,4},{6,7},{7,6},{8,9},{9,8},{10,11... | collective-permute-start | bytes 6291464 | tf_op jit(solution)/shard_map/ppermute | solution.py:469
  101.8 69.5 %collective-permute-start.7 = (f32[512,1024]{1,0:T(8,128)}, f32[512,1024]{1,0:T(8,128)}, u32[]{:S(2)}, u32[]{:S(2)}) collective-permute-start(f32[512,1024]{1,0:T(8,128)} %collective-permute-done.6.refs_1_), channel_id=1, source_target_pairs={{0,1},{1,0},{2,3},{3,2},{4,5},{5,4},{6,7},{7,6},{8,9},{9,8},{10,11... | collective-permute-start | bytes 6291464 | tf_op jit(solution)/shard_map/ppermute | solution.py:469
  136.0 35.3 %collective-permute-start.10 = (f32[256,1024]{1,0:T(8,128)}, f32[256,1024]{1,0:T(8,128)}, u32[]{:S(2)}, u32[]{:S(2)}) collective-permute-start(f32[256,1024]{1,0:T(8,128)} %collective-permute-done.8.refs_2_), channel_id=1, source_target_pairs={{0,1},{1,0},{2,3},{3,2},{4,5},{5,4},{6,7},{7,6},{8,9},{9,8},{10,11... | collective-permute-start | bytes 3145736 | tf_op jit(solution)/shard_map/ppermute | solution.py:469
  136.1 35.2 %collective-permute-start.11 = (f32[256,1024]{1,0:T(8,128)}, f32[256,1024]{1,0:T(8,128)}, u32[]{:S(2)}, u32[]{:S(2)}) collective-permute-start(f32[256,1024]{1,0:T(8,128)} %collective-permute-done.9.refs_3_), channel_id=1, source_target_pairs={{0,1},{1,0},{2,3},{3,2},{4,5},{5,4},{6,7},{7,6},{8,9},{9,8},{10,11... | collective-permute-start | bytes 3145736 | tf_op jit(solution)/shard_map/ppermute | solution.py:469
  194.5 80.0 %collective-permute-start.13 = (f32[1024,1536]{1,0:T(8,128)}, f32[1024,1536]{1,0:T(8,128)}, u32[]{:S(2)}, u32[]{:S(2)}) collective-permute-start(f32[1024,1536]{1,0:T(8,128)} %get-tuple-element.42), channel_id=1, source_target_pairs={{0,1},{1,0},{2,3},{3,2},{4,5},{5,4},{6,7},{7,6},{8,9},{9,8},{10,11... | collective-permute-start | bytes 18874376 | tf_op jit(solution)/shard_map/ppermute | solution.py:469
  215.7 87.8 %collective-permute-start.14 = (f32[1024,1536]{1,0:T(8,128)}, f32[1024,1536]{1,0:T(8,128)}, u32[]{:S(2)}, u32[]{:S(2)}) collective-permute-start(f32[1024,1536]{1,0:T(8,128)} %get-tuple-element.44), channel_id=1, source_target_pairs={{0,1},{1,0},{2,3},{3,2},{4,5},{5,4},{6,7},{7,6},{8,9},{9,8},{10,11... | collective-permute-start | bytes 18874376 | tf_op jit(solution)/shard_map/ppermute | solution.py:469
  216.2 47.8 %collective-permute-start = (f32[512,1024]{1,0:T(8,128)}, f32[512,1024]{1,0:T(8,128)S(1)}, u32[]{:S(2)}, u32[]{:S(2)}) collective-permute-start(f32[512,1024]{1,0:T(8,128)} %get-tuple-element.30.da_ref), channel_id=1, source_target_pairs={{0,8},{8,0},{1,9},{9,1},{2,10},{10,2},{3,11},{11,3},{4,12},{12,4},... | collective-permute-start | bytes 6291464 | tf_op jit(solution)/shard_map/ppermute | solution.py:487
  264.0 1.3 copy-start
  268.2 1.2 collective-permute-start.1
  269.5 3.7 collective-permute-start.2
  273.3 98.6 %collective-permute-start.3 = (f32[3,1024]{1,0:T(4,128)S(1)}, f32[3,1024]{1,0:T(4,128)S(1)}, u32[]{:S(2)}, u32[]{:S(2)}) collective-permute-start(f32[3,1024]{1,0:T(4,128)S(1)} %fusion.2), channel_id=1, source_target_pairs={{0,4},{1,5},{2,6},{3,7},{4,0},{5,1},{6,2},{7,3},{8,12},{9,13},{10,... | collective-permute-start | bytes 36872 | tf_op jit(solution)/shard_map/ppermute | solution.py:469
  326.7 48.5 %collective-permute-start.16 = (f32[1024,1024]{1,0:T(8,128)}, f32[1024,1024]{1,0:T(8,128)}, u32[]{:S(2)}, u32[]{:S(2)}) collective-permute-start(f32[1024,1024]{1,0:T(8,128)} %get-tuple-element.47), channel_id=1, source_target_pairs={{0,1},{1,0},{2,3},{3,2},{4,5},{5,4},{6,7},{7,6},{8,9},{9,8},{10,11... | collective-permute-start | bytes 12582920 | tf_op jit(solution)/shard_map/ppermute | solution.py:469
  326.7 48.4 %collective-permute-start.15 = (f32[1024,1536]{1,0:T(8,128)}, f32[1024,1536]{1,0:T(8,128)}, u32[]{:S(2)}, u32[]{:S(2)}) collective-permute-start(f32[1024,1536]{1,0:T(8,128)} %get-tuple-element.46), channel_id=1, source_target_pairs={{0,1},{1,0},{2,3},{3,2},{4,5},{5,4},{6,7},{7,6},{8,9},{9,8},{10,11... | collective-permute-start | bytes 18874376 | tf_op jit(solution)/shard_map/ppermute | solution.py:469
  327.2 45.8 %copy-start.3 = (f32[1,1536]{1,0:T(1,128)S(1)}, f32[1,1536]{1,0:T(1,128)}, u32[]{:S(2)}) copy-start(f32[1,1536]{1,0:T(1,128)} %get-tuple-element.49) | copy-start | bytes 18436
  327.2 45.8 %copy-start.2 = (f32[1,1536]{1,0:T(1,128)S(1)}, f32[1,1536]{1,0:T(1,128)}, u32[]{:S(2)}) copy-start(f32[1,1536]{1,0:T(1,128)} %get-tuple-element.48) | copy-start | bytes 18436
  327.2 45.9 %copy-start.4 = (f32[1,1536]{1,0:T(1,128)S(1)}, f32[1,1536]{1,0:T(1,128)}, u32[]{:S(2)}) copy-start(f32[1,1536]{1,0:T(1,128)} %get-tuple-element.50) | copy-start | bytes 18436
  327.3 45.9 %copy-start.1 = (f32[1,1024]{1,0:T(1,128)S(1)}, f32[1,1024]{1,0:T(1,128)}, u32[]{:S(2)}) copy-start(f32[1,1024]{1,0:T(1,128)} %get-tuple-element.51) | copy-start | bytes 12292
  373.2 1.2 collective-permute-start.17

commit v3 on v2

v3 whole, which is shorter than its diff:
```python
import functools

import jax
import jax.numpy as jnp
from jax import lax
from jax.experimental import pallas as pl
from jax.experimental.pallas import tpu as pltpu
from jax.sharding import PartitionSpec as P


VALID = 21841
LN_EPS = 1e-5
SMOOTH = 0.1
F32 = jnp.float32
BF16 = jnp.bfloat16
MIB = 2**20


def _cost(flops, nbytes):
    return pl.CostEstimate(flops=int(flops), bytes_accessed=int(nbytes), transcendentals=0)


def _ln_kernel(f_ref, g_ref, b_ref, p_ref, xm_ref, mean_ref, inv_ref, *, rows, sub):
    lane = lax.broadcasted_iota(jnp.int32, (sub, 128), 1)
    tokens, _, width = f_ref.shape

    def step(s, carry):
        r = pl.ds(pl.multiple_of(s * sub, sub), sub)
        acc = jnp.zeros((sub, width), F32)
        means = jnp.zeros((sub, 128), F32)
        invs = jnp.zeros((sub, 128), F32)
        for t in range(tokens):
            x = f_ref[t, r, :].astype(F32)
            mu = jnp.sum(x, -1, keepdims=True) * (1.0 / width)
            xc = x - mu
            iv = lax.rsqrt(jnp.sum(xc * xc, -1, keepdims=True) * (1.0 / width) + LN_EPS)
            acc = acc + xc * iv
            means = jnp.where(lane == t, mu, means)
            invs = jnp.where(lane == t, iv, invs)
        xm = acc * (1.0 / tokens)
        xm_ref[r, :] = xm
        p_ref[r, :] = (xm * g_ref[...] + b_ref[...]).astype(BF16).astype(F32)
        mean_ref[r, :] = means
        inv_ref[r, :] = invs
        return carry

    lax.fori_loop(0, rows // sub, step, 0)


def _ln_forward(ft, gamma, beta, rows=64, sub=16):
    tokens, images, width = ft.shape
    return pl.pallas_call(
        functools.partial(_ln_kernel, rows=rows, sub=sub),
        grid=(images // rows,),
        in_specs=[
            pl.BlockSpec((tokens, rows, width), lambda i: (0, i, 0)),
            pl.BlockSpec((1, width), lambda i: (0, 0)),
            pl.BlockSpec((1, width), lambda i: (0, 0)),
        ],
        out_specs=[pl.BlockSpec((rows, width), lambda i: (i, 0))] * 2 + [pl.BlockSpec((rows, 128), lambda i: (i, 0))] * 2,
        out_shape=[jax.ShapeDtypeStruct((images, width), F32)] * 2 + [jax.ShapeDtypeStruct((images, 128), F32)] * 2,
        compiler_params=pltpu.CompilerParams(vmem_limit_bytes=60 * MIB),
        cost_estimate=_cost(36e-6 * 996e12, tokens * images * width * 2),
        name="ln_forward",
    )(ft, gamma, beta)


def _df_rows(f_ref, da_ref, db_ref, g_ref, mean_ref, inv_ref, o_ref, mu_all, iv_all, r, group=7):
    tokens, _, width = f_ref.shape
    lanes = [slice(k * 128, (k + 1) * 128) for k in range(width // 128)]
    up = (da_ref[r, :] + db_ref[r, :]) * g_ref[...] * (1.0 / tokens)
    up = up - jnp.mean(up, -1, keepdims=True)
    means = mean_ref[r, :]
    invs = inv_ref[r, :]
    spread = (up.shape[0], 128)
    for t in range(tokens):
        mu_all[t, r, :] = jnp.broadcast_to(means[:, t : t + 1], spread)
        iv_all[t, r, :] = jnp.broadcast_to(invs[:, t : t + 1], spread)
    for t0 in range(0, tokens, group):
        scales = []
        for t in range(t0, t0 + group):
            x = f_ref[t, r, :].astype(F32)
            mu, iv = mu_all[t, r, :], iv_all[t, r, :]
            q = jnp.zeros(spread, F32)
            for c in lanes:
                q = q + (x[:, c] - mu) * up[:, c]
            proj = jnp.sum(q, -1, keepdims=True) * (1.0 / width)
            scales.append(proj * iv * iv * iv)
        for t in range(t0, t0 + group):
            x = f_ref[t, r, :].astype(F32)
            mu, iv, k = mu_all[t, r, :], iv_all[t, r, :], scales[t - t0]
            o_ref[t, r, :] = jnp.concatenate([iv * up[:, c] - (x[:, c] - mu) * k for c in lanes], 1).astype(BF16)


def _masked(w, bias, col):
    valid = col < VALID
    return jnp.where(valid, w, jnp.zeros((), BF16)), jnp.where(valid, bias, -1e30)


def _dlogit(logit, shift, col, y, total):
    flat = jnp.where(col < VALID, SMOOTH / VALID / total, 0.0)
    drop = jnp.where(col == y, (SMOOTH / VALID + 1.0 - SMOOTH) / total, flat)
    return jnp.exp(logit - shift) - drop


def _rows_to_columns(rows):
    return jnp.concatenate([rows] * 16, 0).T


def _head_kernel(p_ref, w_ref, b_ref, y_ref, o_ref, sh_ref, loss_ref, l_all, m_acc, s_acc, t_acc, v_acc, p16, mine, other, send, every, shift, zs, zr, ds, dr, *, tile, steps, row_block, total, dp_size):
    i = pl.program_id(0)
    tp_i, dp_i = lax.axis_index("tp"), lax.axis_index("dp")
    images = p16.shape[0]
    t = lax.rem(i, steps)
    col = tp_i * (tile * steps) + t * tile + lax.broadcasted_iota(jnp.int32, (1, tile), 1)
    lane = lax.broadcasted_iota(jnp.int32, (1, 128), 1)
    barrier = pltpu.get_barrier_semaphore()
    mesh_id = pl.DeviceIdType.MESH
    across = pltpu.make_async_remote_copy(mine, other, zs, zr, device_id=(1 - tp_i, dp_i), device_id_type=mesh_id)
    casts = [
        pltpu.make_async_remote_copy(
            send, every.at[dp_i], ds.at[j], dr.at[j], device_id=(tp_i, lax.rem(dp_i + j + 1, dp_size)), device_id_type=mesh_id
        )
        for j in range(dp_size - 1)
    ]

    @pl.when(i == 0)
    def _():
        pl.semaphore_signal(barrier, inc=1, device_id=(1 - tp_i, dp_i), device_id_type=mesh_id)
        for j in range(dp_size - 1):
            pl.semaphore_signal(barrier, inc=1, device_id=(tp_i, lax.rem(dp_i + j + 1, dp_size)), device_id_type=mesh_id)
        m_acc[...] = jnp.full(m_acc.shape, -jnp.inf, F32)
        for acc in (s_acc, t_acc, v_acc):
            acc[...] = jnp.zeros(acc.shape, F32)
        p16[...] = p_ref[...].astype(BF16)

    @pl.when(i < steps)
    def _():
        w, bias = _masked(w_ref[...], b_ref[...], col)
        groups = [slice(k * 128, (k + 1) * 128) for k in range(tile // 128)]
        bsum = jnp.zeros((1, 128), F32)
        kept = jnp.where(col < VALID, b_ref[...], 0.0)
        for g in groups:
            bsum = bsum + kept[:, g]
        for r0 in range(0, images, row_block):
            r = slice(r0, r0 + row_block)
            raw = jnp.dot(p16[r, :], w, preferred_element_type=F32)
            logit = raw + bias
            l_all[t, r, :] = logit
            target = jnp.where(col == y_ref[r, :], logit, 0.0)
            m0 = m_acc[r, :]
            m = m0
            for g in groups:
                m = jnp.maximum(m, logit[:, g])
            s = s_acc[r, :] * jnp.exp(m0 - m)
            tt, v = t_acc[r, :], v_acc[r, :] + bsum
            for g in groups:
                s = s + jnp.exp(logit[:, g] - m)
                tt = tt + target[:, g]
                v = v + raw[:, g]
            m_acc[r, :] = m
            s_acc[r, :] = s
            t_acc[r, :] = tt
            v_acc[r, :] = v

    @pl.when(i == steps - 1)
    def _():
        m = m_acc[...]
        top = jnp.max(m, -1, keepdims=True)
        norm = jnp.sum(s_acc[...] * jnp.exp(m - top), -1, keepdims=True)
        target = jnp.sum(t_acc[...], -1, keepdims=True)
        valid_sum = jnp.sum(v_acc[...], -1, keepdims=True)
        stats = jnp.where(lane == 0, top, jnp.where(lane == 1, norm, jnp.where(lane == 2, target, valid_sum)))
        mine[...] = stats.T[:8, :]

    @pl.when(i == steps)
    def _():
        pl.semaphore_wait(barrier, dp_size)
        across.start()
        across.wait()
        a, b = mine[...], other[...]
        top = jnp.maximum(a[0:1], b[0:1])
        lse = top + jnp.log(a[1:2] * jnp.exp(a[0:1] - top) + b[1:2] * jnp.exp(b[0:1] - top))
        loss = lse - (1.0 - SMOOTH) * (a[2:3] + b[2:3]) - (SMOOTH / VALID) * (a[3:4] + b[3:4])
        row = lax.broadcasted_iota(jnp.int32, (8, images), 0)
        rows = jnp.where(row == 0, lse + jnp.log(F32(total)), jnp.where(row == 1, loss, 0.0))
        cols = _rows_to_columns(rows)
        shift[...] = cols
        loss_ref[...] = loss
        out = jnp.where(lane == 2, y_ref[...].astype(F32), cols)
        send[...] = out.T[:8, :]

    @pl.when(i == steps + 1)
    def _():
        every[dp_i] = send[...]
        for c in casts:
            c.start()

    @pl.when(i >= steps)
    def _():
        for r0 in range(0, images, row_block):
            r = slice(r0, r0 + row_block)
            d = _dlogit(l_all[t, r, :], shift[r, 0:1], col, y_ref[r, :], total).astype(BF16)
            part = lax.dot_general(d, w_ref[...], (((1,), (1,)), ((), ())), preferred_element_type=F32)
            o_ref[r, :] = jnp.where(i == steps, part, o_ref[r, :] + part)

    @pl.when(i == 2 * steps - 1)
    def _():
        for c in casts:
            c.wait()
        sh_ref[...] = every[...]


def _own_head(p, w, b, y, dp_size, tile=2816, row_block=256):
    images, width = p.shape
    cols = w.shape[1]
    steps = cols // tile
    dma = pltpu.SemaphoreType.DMA
    small = pltpu.VMEM((8, images), F32)
    return pl.pallas_call(
        functools.partial(_head_kernel, tile=tile, steps=steps, row_block=row_block, total=images * dp_size, dp_size=dp_size),
        grid=(2 * steps,),
        in_specs=[
            pl.BlockSpec((images, width), lambda i: (0, 0)),
            pl.BlockSpec((width, tile), lambda i: (0, lax.rem(i, steps))),
            pl.BlockSpec((1, tile), lambda i: (0, lax.rem(i, steps))),
            pl.BlockSpec((images, 1), lambda i: (0, 0)),
        ],
        out_specs=[pl.BlockSpec((images, width), lambda i: (0, 0)), pl.BlockSpec((dp_size, 8, images), lambda i: (0, 0, 0)), pl.BlockSpec((1, images), lambda i: (0, 0))],
        out_shape=[jax.ShapeDtypeStruct((images, width), F32), jax.ShapeDtypeStruct((dp_size, 8, images), F32), jax.ShapeDtypeStruct((1, images), F32)],
        scratch_shapes=[pltpu.VMEM((steps, images, tile), F32)]
        + [pltpu.VMEM((images, 128), F32)] * 4
        + [pltpu.VMEM((images, width), BF16), small, small, small, pltpu.VMEM((dp_size, 8, images), F32), pltpu.VMEM((images, 128), F32)]
        + [dma, dma, dma((dp_size - 1,)), dma((dp_size - 1,))],
        compiler_params=pltpu.CompilerParams(vmem_limit_bytes=60 * MIB, collective_id=0, has_side_effects=True),
        cost_estimate=_cost(4 * images * width * cols, width * cols * 4),
        name="own_head",
    )(p, w, b, y)


DF_ROWS = 48
DF_SUB = 16


def _dw_kernel(sc_ref, *refs, counts, sets, tile, row_block, total, has_acc, aliased, to_full, give_p, off):
    refs = list(refs)
    take = lambda n: [refs.pop(0) for _ in range(n)]
    p_refs = take(len(counts))
    sh_refs = take(sets)
    w_ref, b_ref = take(2)
    acc_ref, acc_db_ref = take(2) if has_acc else (None, None)
    ln_refs = take(6) if to_full else None
    take(2 if aliased else 0)
    full_ref, df_ref = take(2) if to_full else (None, None)
    o_ref, db_ref = take(2)
    (give_ref,) = take(1) if give_p else (None,)
    d16, stat = take(2)
    mu_all, iv_all = take(2) if to_full else (None, None)
    p16 = refs[0] if refs else p_refs[0]
    images = d16.shape[0]
    i = pl.program_id(0)

    @pl.when(i == 0)
    def _():
        if p16 is not p_refs[0]:
            r0 = 0
            for ref, n in zip(p_refs, counts):
                p16[r0 : r0 + n, :] = ref[...].astype(BF16)
                r0 += n
            if give_p:
                give_ref[...] = p16[...]
        n = images // sets
        for k, ref in enumerate(sh_refs):
            stat[k * n : (k + 1) * n, :] = _rows_to_columns(ref[0])

    col = sc_ref[0] + (off + i) * tile + lax.broadcasted_iota(jnp.int32, (1, tile), 1)
    w, bias = _masked(w_ref[...], b_ref[...], col)
    db = jnp.zeros((1, tile), F32)
    for r0 in range(0, images, row_block):
        r = slice(r0, r0 + row_block)
        logit = jnp.dot(p16[r, :], w, preferred_element_type=F32) + bias
        d = _dlogit(logit, stat[r, 0:1], col, stat[r, 2:3].astype(jnp.int32), total)
        db = db + jnp.sum(d, 0, keepdims=True)
        d16[r, :] = d.astype(BF16)
    if to_full:
        for r0 in range(0, DF_ROWS, DF_SUB):
            _df_rows(*ln_refs, df_ref, mu_all, iv_all, slice(r0, r0 + DF_SUB))
    out = lax.dot_general(p16[...], d16[...], (((0,), (0,)), ((), ())), preferred_element_type=F32)
    if has_acc:
        out = out + acc_ref[...]
        db = db + acc_db_ref[...]
    o_ref[...] = out
    if to_full:
        full_ref[...] = out
    db_ref[...] = db


def _dw_phase(sc, pooled, slots, shifts, w, b, total, acc=None, own=None, off=0, ln=None, so_far=None, give_p=False, tile=512, row_block=512):
    counts = [p.shape[0] for p in pooled]
    images = sum(counts)
    width, cols = w.shape
    own = own or cols // 2 // tile
    const = lambda shape: pl.BlockSpec(shape, lambda i, s: (0, 0))
    in_specs = [const(p.shape) for p in pooled]
    in_specs += [pl.BlockSpec((1, *shifts.shape[1:]), lambda i, s, k=k: (s[3 + k], 0, 0)) for k in slots]
    in_specs += [pl.BlockSpec((width, tile), lambda i, s: (0, s[1] + off + i)), pl.BlockSpec((1, tile), lambda i, s: (0, s[1] + off + i))]
    args = list(pooled) + [shifts] * len(slots) + [w, b]
    if acc is not None:
        in_specs += [pl.BlockSpec((width, tile), lambda i, s: (0, off + i)), pl.BlockSpec((1, tile), lambda i, s: (0, off + i))]
        args += list(acc)
    out_specs = [pl.BlockSpec((width, tile), lambda i, s: (0, i)), pl.BlockSpec((1, tile), lambda i, s: (0, i))]
    out_shape = [jax.ShapeDtypeStruct((width, own * tile), F32), jax.ShapeDtypeStruct((1, own * tile), F32)]
    scratch = [pltpu.VMEM((images, tile), BF16), pltpu.VMEM((images, 128), F32)]
    aliases = {}
    flops, nbytes = 4.6 * images * width * own * tile, width * own * tile * 10
    if ln is not None:
        tokens = ln[0].shape[0]
        f_block = pl.BlockSpec((tokens, DF_ROWS, width), lambda i, s: (0, off + i, 0))
        rows = pl.BlockSpec((DF_ROWS, width), lambda i, s: (off + i, 0))
        stats = pl.BlockSpec((DF_ROWS, 128), lambda i, s: (off + i, 0))
        in_specs += [f_block, rows, rows, const((1, width)), stats, stats]
        args += list(ln)
        if so_far is not None:
            aliases = {len(args) + 1: 0, len(args) + 2: 1}
            in_specs += [pl.BlockSpec(memory_space=pl.ANY)] * 2
            args += list(so_far)
        out_specs = [pl.BlockSpec((width, tile), lambda i, s: (0, s[1] + off + i)), f_block] + out_specs
        out_shape = [jax.ShapeDtypeStruct((width, cols), F32), jax.ShapeDtypeStruct(ln[0].shape, BF16)] + out_shape
        scratch += [pltpu.VMEM((tokens, DF_ROWS, 128), F32)] * 2
        nbytes += own * DF_ROWS * tokens * width * 4
    if give_p:
        out_specs.append(const((images, width)))
        out_shape.append(jax.ShapeDtypeStruct((images, width), BF16))
    if pooled[0].dtype != BF16:
        scratch.append(pltpu.VMEM((images, width), BF16))
    return pl.pallas_call(
        functools.partial(
            _dw_kernel,
            counts=counts,
            sets=len(slots),
            tile=tile,
            row_block=row_block,
            total=total,
            has_acc=acc is not None,
            aliased=so_far is not None,
            to_full=ln is not None,
            give_p=give_p,
            off=off,
        ),
        grid_spec=pltpu.PrefetchScalarGridSpec(num_scalar_prefetch=1, grid=(own,), in_specs=in_specs, out_specs=out_specs, scratch_shapes=scratch),
        out_shape=out_shape,
        input_output_aliases=aliases,
        compiler_params=pltpu.CompilerParams(vmem_limit_bytes=67043328),
        cost_estimate=_cost(flops, nbytes),
        name="dw_phase",
    )(sc, *args)


def _place_kernel(sc_ref, full_in, *refs, pieces, slots, tile):
    *parts, full_ref, buf, in_sem, out_sem = refs
    height = buf.shape[1]
    ins, outs = [], []
    for k, (part, row, src, dst) in enumerate(pieces):
        slot = k % slots
        rows = pl.ds(row * height, height)
        col = pl.multiple_of((sc_ref[2] + dst) * tile, tile)
        ins.append(pltpu.make_async_copy(parts[part].at[rows, pl.ds(src * tile, tile)], buf.at[slot], in_sem.at[slot]))
        outs.append(pltpu.make_async_copy(buf.at[slot], full_ref.at[rows, pl.ds(col, tile)], out_sem.at[slot]))
    n, half = len(pieces), slots // 2
    for k in range(min(half, n)):
        ins[k].start()
    for k in range(n):
        ins[k].wait()
        outs[k].start()
        ahead = k + half
        if ahead < n:
            if ahead >= slots:
                outs[ahead - slots].wait()
            ins[ahead].start()
    for k in range(max(0, n - slots), n):
        outs[k].wait()


def _place(sc, full, parts, off, tile=512, split=4, slots=24):
    width = full.shape[0]
    pieces, dst = [], off
    for k, part in enumerate(parts):
        for src in range(part.shape[1] // tile):
            pieces += [(k, row, src, dst) for row in range(split)]
            dst += 1
    anywhere = pl.BlockSpec(memory_space=pl.ANY)
    return pl.pallas_call(
        functools.partial(_place_kernel, pieces=pieces, slots=slots, tile=tile),
        grid_spec=pltpu.PrefetchScalarGridSpec(
            num_scalar_prefetch=1,
            grid=(1,),
            in_specs=[anywhere] * (1 + len(parts)),
            out_specs=anywhere,
            scratch_shapes=[pltpu.VMEM((slots, width // split, tile), F32), pltpu.SemaphoreType.DMA((slots,)), pltpu.SemaphoreType.DMA((slots,))],
        ),
        out_shape=jax.ShapeDtypeStruct(full.shape, F32),
        input_output_aliases={1: 0},
        compiler_params=pltpu.CompilerParams(vmem_limit_bytes=60 * MIB),
        cost_estimate=_cost(6e-6 * 996e12, 8 * tile * width * (dst - off)),
        name="place",
    )(sc, full, *parts)


CHUNKS = (8, 3)
TILE = 512


def solution(mesh):
    dp_size, tp_size = mesh.shape["dp"], mesh.shape["tp"]

    def swap(x, bit):
        return lax.ppermute(x, "dp", [(i, i ^ bit) for i in range(dp_size)])

    def head(feats, ln_gamma, ln_beta, w, b, labels):
        images, _, width = feats.shape
        cols = w.shape[1]
        total = images * dp_size
        tp_i, dp_i = lax.axis_index("tp"), lax.axis_index("dp")
        core = dp_i % 2
        half_tiles = cols // 2 // TILE
        bits = (0, 1, 2, 4, 3, 5, 6, 7)
        sc = jnp.stack([tp_i * cols + core * (cols // 2), core * half_tiles, (1 - core) * half_tiles] + [dp_i ^ k for k in bits]).astype(jnp.int32)
        ft = jnp.transpose(feats, (1, 0, 2))
        gamma, beta, bias = ln_gamma.reshape(1, width), ln_beta.reshape(1, width), b.reshape(1, cols)

        p, xm, means, invs = _ln_forward(ft, gamma, beta)
        p_x, p_y, p_core = swap(p, 2), swap(p, 4), swap(p, 1)

        dpool_a, shifts, loss_rows = _own_head(p, w, bias, labels.reshape(images, 1), dp_size)
        p_d = swap(lax.optimization_barrier((p, loss_rows))[0], 6)
        dpool_b = lax.ppermute(dpool_a, "tp", [(i, tp_size - 1 - i) for i in range(tp_size)])

        acc = _dw_phase(sc, [p, p_core, p_x, p_y], (0, 1, 2, 3), shifts, w, bias, total)
        p_rest = [swap(p_x, 1), swap(p_y, 1), p_d, swap(p_d, 1)]

        so_far, sent, dbs, off = None, [], [], 0
        ln = (ft, dpool_a, dpool_b, gamma, means, invs)
        for c, n in enumerate(CHUNKS):
            full, dft, part, db, *rest = _dw_phase(
                sc, p_rest, (4, 5, 6, 7), shifts, w, bias, total, acc=acc, own=n, off=off, ln=ln, so_far=so_far, give_p=c == 0
            )
            so_far = (full, dft)
            p_rest = rest or p_rest
            sent.append(swap(part, 1))
            dbs.append(db)
            off += n

        db_mine = jnp.concatenate(dbs, 1)
        db_other = swap(db_mine, 1)
        grad_b = jnp.where(core == 0, jnp.concatenate([db_mine, db_other], 1), jnp.concatenate([db_other, db_mine], 1)).reshape(cols)

        dpool = dpool_a + dpool_b
        loss_own = jnp.sum(loss_rows)
        sums = jnp.stack([jnp.sum(dpool * xm, 0), jnp.sum(dpool, 0), jnp.broadcast_to(loss_own / total, (width,))])
        for bit in (1, 2, 4):
            sums = sums + swap(sums, bit)

        full = _place(sc, full, sent[:-1], 0)
        full = _place(sc, full, sent[-1:], off - CHUNKS[-1])
        return sums[2, 0], jnp.transpose(dft, (1, 0, 2)), full, grad_b, sums[0], sums[1]

    return jax.shard_map(
        head,
        mesh=mesh,
        in_specs=(P("dp", None, None), P(), P(), P(None, "tp"), P("tp"), P("dp")),
        out_specs=(P(), P("dp", None, None), P(None, "tp"), P("tp"), P(), P()),
        check_vma=False,
    )
```

time: 387 us -> 369 us (0.953)
  Pallas kernels: 309 us -> 253 us
  waiting for transfers between devices: 48.8 us -> 97.3 us
  starting transfers between devices: 13.3 us -> 7.7 us
  local copies, waits for them, and re-layouts: 8.75 us -> 3.41 us
    ppermute x17 -> x13, waiting for transfers between devices: 4.6 us -> 97.3 us  [swap(): return lax.ppermute(x, 'dp', [(i, i ^ bit) for i in range(dp_size)])]
    ppermute x1, waiting for transfers between devices: 44.2 us -> 0.01 us  [head(): lax.ppermute(dpool_a, 'tp', [(i, tp_size - 1 - i) for i in range(tp_size)])]
    pallas_call x3, Pallas kernels: 96.1 us -> 55.9 us  [the longest x1 36.7 us: _ln_forward(): pl.pallas_call(functools.partial(_ln_kernel, rows=rows, sub=sub), grid=(i...]
    pallas_call x1, Pallas kernels: 47.7 us -> 39.5 us  [_own_head(): pl.pallas_call(functools.partial(_head_kernel, tile=tile, steps=steps, ro...]
    pallas_call x6 -> x3, Pallas kernels: 165 us -> 157 us  [_dw_phase(): pl.pallas_call(functools.partial(_dw_kernel, counts=counts, sets=len(slot...]
    slice x2 -> x0, local copies, waits for them, and re-layouts: 4.71 us -> none  [head(): p_d = [swap(p_x[:half], 4), swap(p_y[half:], 2)]]
    ppermute x17 -> x13, starting transfers between devices: 11.8 us -> 7.68 us  [swap(): return lax.ppermute(x, 'dp', [(i, i ^ bit) for i in range(dp_size)])]
  transfers between devices with their start and end apart: 18 -> 14, of which waited for: 4 -> 6; matrix products, arithmetic and copies ran while one was open for 3% -> 2% of each run, Pallas kernels for 61% -> 28%
where the time goes in v3:
time: 369 us; the launch traced here: 368 us
  Pallas kernels  253 us (69%)
  waiting for transfers between devices  97.3 us (26%)
  starting transfers between devices  7.7 us (2%)
  other arithmetic  5.73 us (2%)
    pallas_call x3, Pallas kernels, _dw_phase(): pl.pallas_call(functools.partial(_dw_kernel, counts=counts, sets=len(slot...  157 us
    ppermute x13, waiting for transfers between devices, swap(): return lax.ppermute(x, 'dp', [(i, i ^ bit) for i in range(dp_size)])  97.3 us
    pallas_call x1, Pallas kernels, _own_head(): pl.pallas_call(functools.partial(_head_kernel, tile=tile, steps=steps, ro...  39.5 us
    pallas_call x1, Pallas kernels, _ln_forward(): pl.pallas_call(functools.partial(_ln_kernel, rows=rows, sub=sub), grid=(i...  36.7 us
    pallas_call x2, Pallas kernels, _place(): pl.pallas_call(functools.partial(_place_kernel, pieces=pieces, slots=slot...  19.2 us
    ppermute x13, starting transfers between devices, swap(): return lax.ppermute(x, 'dp', [(i, i ^ bit) for i in range(dp_size)])  7.68 us
  transfers between devices with their start and end apart: 14, of which 6 were waited for; matrix products, arithmetic and copies ran while one was open for 2% of the time, Pallas kernels for 28%

profile of v3, /device:TPU:0, one launch (start us, length us, event | category | flops | bytes accessed | tf_op | source)
XLA Modules:
  0.0 368.3 jit_solution(7262772472853805103)
XLA Ops:
  0.6 1.5 copy.16.y_ref
  2.2 36.7 %ln_forward.1 = (f32[512,1024]{1,0:T(8,128)}, f32[512,1024]{1,0:T(8,128)}, f32[512,128]{1,0:T(8,128)}, f32[512,128]{1,0:T(8,128)}) custom-call(bf16[49,512,1024]{2,1,0:T(8,128)(2,1)} %bitcast.24, f32[1,1024]{1,0:T(1,128)} %bitcast.39, f32[1,1024]{1,0:T(1,128)} %bitcast.45), custom_call_target="tpu_custom_call" | custom-call | flops 35855998976 | bytes 51380224 | tf_op jit(solution)/shard_map/ln_forward/pallas_call | solution.py:52
  38.9 39.5 %own_head.1 = (f32[512,1024]{1,0:T(8,128)}, f32[8,8,512]{2,1,0:T(8,128)}, f32[1,512]{1,0:T(1,128)}) custom-call(f32[512,1024]{1,0:T(8,128)} %get-tuple-element.29.p_ref.refs_0_, bf16[1024,11264]{1,0:T(8,128)(2,1)} %refs_5_.1, f32[1,11264]{1,0:T(1,128)} %bitcast.35, s32[512,1]{1,0:T(8,128)} %copy.16.y_ref), custom_call_target="tpu_custom_call" | custom-call | flops 23622320128 | bytes 46137344 | tf_op jit(solution)/shard_map/own_head/pallas_call | solution.py:220
  78.4 2.5 collective-permute-start.8
  80.9 0.5 collective-permute-start.6
  81.4 0.5 collective-permute-start.4
  82.0 0.7 stack.59.sc_ref
  82.6 45.4 %collective-permute-done.8.refs_2_ = f32[512,1024]{1,0:T(8,128)} collective-permute-done((f32[512,1024]{1,0:T(8,128)S(1)}, f32[512,1024]{1,0:T(8,128)}, u32[]{:S(2)}, u32[]{:S(2)}) %collective-permute-start.8) | collective-permute-done | bytes 2097184 | tf_op jit(solution)/shard_map/ppermute | solution.py:417
  128.0 42.9 %collective-permute-done.6.refs_3_ = f32[512,1024]{1,0:T(8,128)} collective-permute-done((f32[512,1024]{1,0:T(8,128)S(1)}, f32[512,1024]{1,0:T(8,128)}, u32[]{:S(2)}, u32[]{:S(2)}) %collective-permute-start.6) | collective-permute-done | bytes 2097184 | tf_op jit(solution)/shard_map/ppermute | solution.py:417
  170.9 0.1 collective-permute-done.4.refs_2_
  171.0 0.4 collective-permute-start.5
  171.4 60.9 %dw_phase.3 = (f32[1024,5632]{1,0:T(8,128)}, f32[1,5632]{1,0:T(1,128)}) custom-call(s32[11]{0:T(128)} %stack.59.sc_ref, f32[512,1024]{1,0:T(8,128)} %get-tuple-element.29.p_ref.refs_0_, f32[512,1024]{1,0:T(8,128)} %collective-permute-done.10.refs_1_, f32[512,1024]{1,0:T(8,128)} %collective-permute-done.4.refs_2_, ...), custom_call_target="tpu_custom_call" | custom-call | flops 54331334656 | bytes 57671680 | tf_op jit(solution)/shard_map/dw_phase/pallas_call | solution.py:336
  232.4 66.9 %dw_phase.4 = (f32[1024,11264]{1,0:T(8,128)}, bf16[49,512,1024]{2,1,0:T(8,128)(2,1)}, f32[1024,4096]{1,0:T(8,128)}, f32[1,4096]{1,0:T(1,128)}, bf16[2048,1024]{1,0:T(8,128)(2,1)}) custom-call(s32[11]{0:T(128)} %stack.59.sc_ref, f32[512,1024]{1,0:T(8,128)} %collective-permute-done.5.refs_0_, f32[512,1024]{1,0:T(8,128)} %collective-permute-done.7.refs_1_, ...), custom_call_target="tpu_custom_call" | custom-call | flops 39513698304 | bytes 119013376 | tf_op jit(solution)/shard_map/dw_phase/pallas_call | solution.py:336
  299.3 0.1 collective-permute-start.11
  299.4 29.3 %dw_phase.5 = (f32[1024,11264]{1,0:T(8,128)}, bf16[49,512,1024]{2,1,0:T(8,128)(2,1)}, f32[1024,1536]{1,0:T(8,128)}, f32[1,1536]{1,0:T(1,128)}) custom-call(s32[11]{0:T(128)} %stack.59.sc_ref, bf16[2048,1024]{1,0:T(8,128)(2,1)} %get-tuple-element.35.refs_0_, ...), custom_call_target="tpu_custom_call", output_to_operand_aliasing={{0}: (16, {}), {1}: (17, {})} | custom-call | flops 14817637376 | bytes 44630016 | tf_op jit(solution)/shard_map/dw_phase/pallas_call | solution.py:336
  328.7 0.4 collective-permute-start.12
  329.2 1.3 reduce_sum.29
  331.1 0.1 pad.10.clone
  331.2 3.5 multiply_reduce_fusion
  334.8 0.1 collective-permute-start.1
  334.9 4.4 %collective-permute-done.1 = f32[3,1024]{1,0:T(4,128)S(1)} collective-permute-done((f32[3,1024]{1,0:T(4,128)S(1)}, f32[3,1024]{1,0:T(4,128)S(1)}, u32[]{:S(2)}, u32[]{:S(2)}) %collective-permute-start.1) | collective-permute-done | bytes 12320 | tf_op jit(solution)/shard_map/ppermute | solution.py:417
  339.3 0.1 fusion
  339.4 1.5 collective-permute-start.2
  340.9 2.2 collective-permute-done.2
  343.1 0.1 fusion.2
  343.2 1.5 collective-permute-start.3
  344.7 2.2 collective-permute-done.3
  347.0 0.6 fusion.1
  347.6 0.5 slice.12
  348.3 0.6 maximum_select_fusion
  348.9 12.8 %place.2.full_in = f32[1024,11264]{1,0:T(8,128)} custom-call(s32[11]{0:T(128)} %stack.59.sc_ref, f32[1024,11264]{1,0:T(8,128)} %get-tuple-element.39.full_in, f32[1024,4096]{1,0:T(8,128)} %collective-permute-done.11.refs_0_), custom_call_target="tpu_custom_call", output_to_operand_aliasing={{}: (1, {})} | custom-call | flops 5976000000 | bytes 33554432 | tf_op jit(solution)/shard_map/place/pallas_call | solution.py:392
  361.8 6.4 %place.3 = f32[1024,11264]{1,0:T(8,128)} custom-call(s32[11]{0:T(128)} %stack.59.sc_ref, f32[1024,11264]{1,0:T(8,128)} %place.2.full_in, f32[1024,1536]{1,0:T(8,128)} %collective-permute-done.12.refs_0_), custom_call_target="tpu_custom_call", output_to_operand_aliasing={{}: (1, {})} | custom-call | flops 5976000000 | bytes 12582912 | tf_op jit(solution)/shard_map/place/pallas_call | solution.py:392
  (24 shorter events, 0.3 us)
Async XLA Ops:
  38.9 39.5 %copy-start.2 = (f32[512,1024]{1,0:T(8,128)S(1)}, f32[512,1024]{1,0:T(8,128)}, u32[]{:S(2)}) copy-start(f32[512,1024]{1,0:T(8,128)} %get-tuple-element.29.p_ref.refs_0_) | copy-start | bytes 6291460
  78.4 49.6 %collective-permute-start.8 = (f32[512,1024]{1,0:T(8,128)S(1)}, f32[512,1024]{1,0:T(8,128)}, u32[]{:S(2)}, u32[]{:S(2)}) collective-permute-start(f32[512,1024]{1,0:T(8,128)S(1)} %copy-done.2), channel_id=1, source_target_pairs={{0,6},{1,7},{2,4},{3,5},{4,2},{5,3},{6,0},{7,1},{8,14},{9,15},{10,... | collective-permute-start | bytes 6291464 | tf_op jit(solution)/shard_map/ppermute | solution.py:417
  80.9 90.0 %collective-permute-start.6 = (f32[512,1024]{1,0:T(8,128)S(1)}, f32[512,1024]{1,0:T(8,128)}, u32[]{:S(2)}, u32[]{:S(2)}) collective-permute-start(f32[512,1024]{1,0:T(8,128)S(1)} %copy-done.2), channel_id=1, source_target_pairs={{0,4},{1,5},{2,6},{3,7},{4,0},{5,1},{6,2},{7,3},{8,12},{9,13},{10,... | collective-permute-start | bytes 6291464 | tf_op jit(solution)/shard_map/ppermute | solution.py:417
  81.4 89.6 %collective-permute-start.4 = (f32[512,1024]{1,0:T(8,128)S(1)}, f32[512,1024]{1,0:T(8,128)}, u32[]{:S(2)}, u32[]{:S(2)}) collective-permute-start(f32[512,1024]{1,0:T(8,128)S(1)} %copy-done.2), channel_id=1, source_target_pairs={{0,2},{1,3},{2,0},{3,1},{4,6},{5,7},{6,4},{7,5},{8,10},{9,11},{10,... | collective-permute-start | bytes 6291464 | tf_op jit(solution)/shard_map/ppermute | solution.py:417
  81.9 89.5 %collective-permute-start.10 = (f32[512,1024]{1,0:T(8,128)S(1)}, f32[512,1024]{1,0:T(8,128)}, u32[]{:S(2)}, u32[]{:S(2)}) collective-permute-start(f32[512,1024]{1,0:T(8,128)S(1)} %copy-done.2), channel_id=1, source_target_pairs={{0,1},{1,0},{2,3},{3,2},{4,5},{5,4},{6,7},{7,6},{8,9},{9,8},{10,11... | collective-permute-start | bytes 6291464 | tf_op jit(solution)/shard_map/ppermute | solution.py:417
  81.9 150.4 %collective-permute-start = (f32[512,1024]{1,0:T(8,128)}, f32[512,1024]{1,0:T(8,128)}, u32[]{:S(2)}, u32[]{:S(2)}) collective-permute-start(f32[512,1024]{1,0:T(8,128)} %get-tuple-element.26.refs_13_.refs_10_), channel_id=1, source_target_pairs={{0,8},{8,0},{1,9},{9,1},{2,10},{10,2},{3,11},{11,3},{4,12},{12,4},... | collective-permute-start | bytes 6291464 | tf_op jit(solution)/shard_map/ppermute | solution.py:436
  128.0 104.4 %collective-permute-start.9 = (f32[512,1024]{1,0:T(8,128)}, f32[512,1024]{1,0:T(8,128)}, u32[]{:S(2)}, u32[]{:S(2)}) collective-permute-start(f32[512,1024]{1,0:T(8,128)} %collective-permute-done.8.refs_2_), channel_id=1, source_target_pairs={{0,1},{1,0},{2,3},{3,2},{4,5},{5,4},{6,7},{7,6},{8,9},{9,8},{10,11... | collective-permute-start | bytes 6291464 | tf_op jit(solution)/shard_map/ppermute | solution.py:417
  170.9 61.5 %collective-permute-start.7 = (f32[512,1024]{1,0:T(8,128)}, f32[512,1024]{1,0:T(8,128)}, u32[]{:S(2)}, u32[]{:S(2)}) collective-permute-start(f32[512,1024]{1,0:T(8,128)} %collective-permute-done.6.refs_3_), channel_id=1, source_target_pairs={{0,1},{1,0},{2,3},{3,2},{4,5},{5,4},{6,7},{7,6},{8,9},{9,8},{10,11... | collective-permute-start | bytes 6291464 | tf_op jit(solution)/shard_map/ppermute | solution.py:417
  171.0 61.4 %collective-permute-start.5 = (f32[512,1024]{1,0:T(8,128)}, f32[512,1024]{1,0:T(8,128)}, u32[]{:S(2)}, u32[]{:S(2)}) collective-permute-start(f32[512,1024]{1,0:T(8,128)} %collective-permute-done.4.refs_2_), channel_id=1, source_target_pairs={{0,1},{1,0},{2,3},{3,2},{4,5},{5,4},{6,7},{7,6},{8,9},{9,8},{10,11... | collective-permute-start | bytes 6291464 | tf_op jit(solution)/shard_map/ppermute | solution.py:417
  299.3 49.6 %collective-permute-start.11 = (f32[1024,4096]{1,0:T(8,128)}, f32[1024,4096]{1,0:T(8,128)}, u32[]{:S(2)}, u32[]{:S(2)}) collective-permute-start(f32[1024,4096]{1,0:T(8,128)} %get-tuple-element.40), channel_id=1, source_target_pairs={{0,1},{1,0},{2,3},{3,2},{4,5},{5,4},{6,7},{7,6},{8,9},{9,8},{10,11... | collective-permute-start | bytes 50331656 | tf_op jit(solution)/shard_map/ppermute | solution.py:417
  328.7 33.0 %collective-permute-start.12 = (f32[1024,1536]{1,0:T(8,128)}, f32[1024,1536]{1,0:T(8,128)}, u32[]{:S(2)}, u32[]{:S(2)}) collective-permute-start(f32[1024,1536]{1,0:T(8,128)} %get-tuple-element.41), channel_id=1, source_target_pairs={{0,1},{1,0},{2,3},{3,2},{4,5},{5,4},{6,7},{7,6},{8,9},{9,8},{10,11... | collective-permute-start | bytes 18874376 | tf_op jit(solution)/shard_map/ppermute | solution.py:417
  331.2 15.8 %copy-start = (f32[1,4096]{1,0:T(1,128)S(1)}, f32[1,4096]{1,0:T(1,128)}, u32[]{:S(2)}) copy-start(f32[1,4096]{1,0:T(1,128)} %get-tuple-element.42) | copy-start | bytes 49156
  331.2 15.8 %copy-start.1 = (f32[1,1536]{1,0:T(1,128)S(1)}, f32[1,1536]{1,0:T(1,128)}, u32[]{:S(2)}) copy-start(f32[1,1536]{1,0:T(1,128)} %get-tuple-element.43) | copy-start | bytes 18436
  334.8 4.5 %collective-permute-start.1 = (f32[3,1024]{1,0:T(4,128)S(1)}, f32[3,1024]{1,0:T(4,128)S(1)}, u32[]{:S(2)}, u32[]{:S(2)}) collective-permute-start(f32[3,1024]{1,0:T(4,128)S(1)} %maximum_maximum_fusion), channel_id=1, source_target_pairs={{0,1},{1,0},{2,3},{3,2},{4,5},{5,4},{6,7},{7,6},{8,9},{9,8},{10,11... | collective-permute-start | bytes 36872 | tf_op jit(solution)/shard_map/ppermute | solution.py:417
  339.4 3.7 %collective-permute-start.2 = (f32[3,1024]{1,0:T(4,128)S(1)}, f32[3,1024]{1,0:T(4,128)S(1)}, u32[]{:S(2)}, u32[]{:S(2)}) collective-permute-start(f32[3,1024]{1,0:T(4,128)S(1)} %fusion), channel_id=1, source_target_pairs={{0,2},{1,3},{2,0},{3,1},{4,6},{5,7},{6,4},{7,5},{8,10},{9,11},{10,... | collective-permute-start | bytes 36872 | tf_op jit(solution)/shard_map/ppermute | solution.py:417
  343.2 3.7 %collective-permute-start.3 = (f32[3,1024]{1,0:T(4,128)S(1)}, f32[3,1024]{1,0:T(4,128)S(1)}, u32[]{:S(2)}, u32[]{:S(2)}) collective-permute-start(f32[3,1024]{1,0:T(4,128)S(1)} %fusion.2), channel_id=1, source_target_pairs={{0,4},{1,5},{2,6},{3,7},{4,0},{5,1},{6,2},{7,3},{8,12},{9,13},{10,... | collective-permute-start | bytes 36872 | tf_op jit(solution)/shard_map/ppermute | solution.py:417
  347.0 1.2 collective-permute-start.13

commit v4 on v3

--- a/solution.py
+++ b/solution.py
@@ -47,7 +47,7 @@
     lax.fori_loop(0, rows // sub, step, 0)
 
 
-def _ln_forward(ft, gamma, beta, rows=64, sub=16):
+def _ln_forward(ft, gamma, beta, rows=32, sub=16):
     tokens, images, width = ft.shape
     return pl.pallas_call(
         functools.partial(_ln_kernel, rows=rows, sub=sub),
@@ -72,6 +72,7 @@
     up = up - jnp.mean(up, -1, keepdims=True)
     means = mean_ref[r, :]
     invs = inv_ref[r, :]
+    up_sum = jnp.sum(up, -1, keepdims=True)
     spread = (up.shape[0], 128)
     for t in range(tokens):
         mu_all[t, r, :] = jnp.broadcast_to(means[:, t : t + 1], spread)
@@ -83,8 +84,8 @@
             mu, iv = mu_all[t, r, :], iv_all[t, r, :]
             q = jnp.zeros(spread, F32)
             for c in lanes:
-                q = q + (x[:, c] - mu) * up[:, c]
-            proj = jnp.sum(q, -1, keepdims=True) * (1.0 / width)
+                q = q + x[:, c] * up[:, c]
+            proj = (jnp.sum(q, -1, keepdims=True) - mu * up_sum) * (1.0 / width)
             scales.append(proj * iv * iv * iv)
         for t in range(t0, t0 + group):
             x = f_ref[t, r, :].astype(F32)
@@ -254,7 +255,7 @@
     full_ref, df_ref = take(2) if to_full else (None, None)
     o_ref, db_ref = take(2)
     (give_ref,) = take(1) if give_p else (None,)
-    d16, stat = take(2)
+    d16, shift_all, y_all = take(3)
     mu_all, iv_all = take(2) if to_full else (None, None)
     p16 = refs[0] if refs else p_refs[0]
     images = d16.shape[0]
@@ -271,7 +272,9 @@
                 give_ref[...] = p16[...]
         n = images // sets
         for k, ref in enumerate(sh_refs):
-            stat[k * n : (k + 1) * n, :] = _rows_to_columns(ref[0])
+            r, cols = slice(k * n, (k + 1) * n), _rows_to_columns(ref[0])
+            shift_all[r, :] = jnp.broadcast_to(cols[:, 0:1], (n, 128))
+            y_all[r, :] = jnp.broadcast_to(cols[:, 2:3], (n, 128)).astype(jnp.int32)
 
     col = sc_ref[0] + (off + i) * tile + lax.broadcasted_iota(jnp.int32, (1, tile), 1)
     w, bias = _masked(w_ref[...], b_ref[...], col)
@@ -279,7 +282,8 @@
     for r0 in range(0, images, row_block):
         r = slice(r0, r0 + row_block)
         logit = jnp.dot(p16[r, :], w, preferred_element_type=F32) + bias
-        d = _dlogit(logit, stat[r, 0:1], col, stat[r, 2:3].astype(jnp.int32), total)
+        wide = lambda a: jnp.concatenate([a] * (tile // 128), 1)
+        d = _dlogit(logit, wide(shift_all[r, :]), col, wide(y_all[r, :]), total)
         db = db + jnp.sum(d, 0, keepdims=True)
         d16[r, :] = d.astype(BF16)
     if to_full:
@@ -310,7 +314,7 @@
         args += list(acc)
     out_specs = [pl.BlockSpec((width, tile), lambda i, s: (0, i)), pl.BlockSpec((1, tile), lambda i, s: (0, i))]
     out_shape = [jax.ShapeDtypeStruct((width, own * tile), F32), jax.ShapeDtypeStruct((1, own * tile), F32)]
-    scratch = [pltpu.VMEM((images, tile), BF16), pltpu.VMEM((images, 128), F32)]
+    scratch = [pltpu.VMEM((images, tile), BF16), pltpu.VMEM((images, 128), F32), pltpu.VMEM((images, 128), jnp.int32)]
     aliases = {}
     flops, nbytes = 4.6 * images * width * own * tile, width * own * tile * 10
     if ln is not None:

time: 369 us -> 362 us (0.981)
  Pallas kernels: 253 us -> 246 us
    pallas_call x3, Pallas kernels: 157 us -> 151 us  [_dw_phase(): pl.pallas_call(functools.partial(_dw_kernel, counts=counts, sets=len(slot...]
where the time goes in v4:
time: 362 us; the launch traced here: 361 us
  Pallas kernels  246 us (68%)
  waiting for transfers between devices  97.3 us (27%)
  starting transfers between devices  7.71 us (2%)
  other arithmetic  5.73 us (2%)
    pallas_call x3, Pallas kernels, _dw_phase(): pl.pallas_call(functools.partial(_dw_kernel, counts=counts, sets=len(slot...  151 us
    ppermute x13, waiting for transfers between devices, swap(): return lax.ppermute(x, 'dp', [(i, i ^ bit) for i in range(dp_size)])  97.3 us
    pallas_call x1, Pallas kernels, _own_head(): pl.pallas_call(functools.partial(_head_kernel, tile=tile, steps=steps, ro...  39.5 us
    pallas_call x1, Pallas kernels, _ln_forward(): pl.pallas_call(functools.partial(_ln_kernel, rows=rows, sub=sub), grid=(i...  36 us
    pallas_call x2, Pallas kernels, _place(): pl.pallas_call(functools.partial(_place_kernel, pieces=pieces, slots=slot...  19.2 us
    ppermute x13, starting transfers between devices, swap(): return lax.ppermute(x, 'dp', [(i, i ^ bit) for i in range(dp_size)])  7.69 us
  transfers between devices with their start and end apart: 14, of which 6 were waited for; matrix products, arithmetic and copies ran while one was open for 2% of the time, Pallas kernels for 28%

profile of v4, /device:TPU:0, one launch (start us, length us, event | category | flops | bytes accessed | tf_op | source)
XLA Modules:
  0.0 361.3 jit_solution(15981077165457697807)
XLA Ops:
  0.6 1.5 copy.16.y_ref
  2.2 36.0 %ln_forward.1 = (f32[512,1024]{1,0:T(8,128)}, f32[512,1024]{1,0:T(8,128)}, f32[512,128]{1,0:T(8,128)}, f32[512,128]{1,0:T(8,128)}) custom-call(bf16[49,512,1024]{2,1,0:T(8,128)(2,1)} %bitcast.24, f32[1,1024]{1,0:T(1,128)} %bitcast.39, f32[1,1024]{1,0:T(1,128)} %bitcast.45), custom_call_target="tpu_custom_call" | custom-call | flops 35855998976 | bytes 51380224 | tf_op jit(solution)/shard_map/ln_forward/pallas_call | solution.py:52
  38.2 39.5 %own_head.1 = (f32[512,1024]{1,0:T(8,128)}, f32[8,8,512]{2,1,0:T(8,128)}, f32[1,512]{1,0:T(1,128)}) custom-call(f32[512,1024]{1,0:T(8,128)} %get-tuple-element.29.p_ref.refs_0_, bf16[1024,11264]{1,0:T(8,128)(2,1)} %refs_5_.1, f32[1,11264]{1,0:T(1,128)} %bitcast.35, s32[512,1]{1,0:T(8,128)} %copy.16.y_ref), custom_call_target="tpu_custom_call" | custom-call | flops 23622320128 | bytes 46137344 | tf_op jit(solution)/shard_map/own_head/pallas_call | solution.py:221
  77.7 2.5 collective-permute-start.8
  80.2 0.5 collective-permute-start.6
  80.7 0.5 collective-permute-start.4
  81.3 0.7 stack.59.sc_ref
  82.0 45.4 %collective-permute-done.8.refs_2_ = f32[512,1024]{1,0:T(8,128)} collective-permute-done((f32[512,1024]{1,0:T(8,128)S(1)}, f32[512,1024]{1,0:T(8,128)}, u32[]{:S(2)}, u32[]{:S(2)}) %collective-permute-start.8) | collective-permute-done | bytes 2097184 | tf_op jit(solution)/shard_map/ppermute | solution.py:421
  127.3 42.9 %collective-permute-done.6.refs_3_ = f32[512,1024]{1,0:T(8,128)} collective-permute-done((f32[512,1024]{1,0:T(8,128)S(1)}, f32[512,1024]{1,0:T(8,128)}, u32[]{:S(2)}, u32[]{:S(2)}) %collective-permute-start.6) | collective-permute-done | bytes 2097184 | tf_op jit(solution)/shard_map/ppermute | solution.py:421
  170.2 0.1 collective-permute-done.4.refs_2_
  170.3 0.4 collective-permute-start.5
  170.7 58.2 %dw_phase.3 = (f32[1024,5632]{1,0:T(8,128)}, f32[1,5632]{1,0:T(1,128)}) custom-call(s32[11]{0:T(128)} %stack.59.sc_ref, f32[512,1024]{1,0:T(8,128)} %get-tuple-element.29.p_ref.refs_0_, f32[512,1024]{1,0:T(8,128)} %collective-permute-done.10.refs_1_, f32[512,1024]{1,0:T(8,128)} %collective-permute-done.4.refs_2_, ...), custom_call_target="tpu_custom_call" | custom-call | flops 54331334656 | bytes 57671680 | tf_op jit(solution)/shard_map/dw_phase/pallas_call | solution.py:340
  229.0 64.0 %dw_phase.4 = (f32[1024,11264]{1,0:T(8,128)}, bf16[49,512,1024]{2,1,0:T(8,128)(2,1)}, f32[1024,4096]{1,0:T(8,128)}, f32[1,4096]{1,0:T(1,128)}, bf16[2048,1024]{1,0:T(8,128)(2,1)}) custom-call(s32[11]{0:T(128)} %stack.59.sc_ref, f32[512,1024]{1,0:T(8,128)} %collective-permute-done.5.refs_0_, f32[512,1024]{1,0:T(8,128)} %collective-permute-done.7.refs_1_, ...), custom_call_target="tpu_custom_call" | custom-call | flops 39513698304 | bytes 119013376 | tf_op jit(solution)/shard_map/dw_phase/pallas_call | solution.py:340
  293.1 0.1 collective-permute-start.11
  293.2 28.5 %dw_phase.5 = (f32[1024,11264]{1,0:T(8,128)}, bf16[49,512,1024]{2,1,0:T(8,128)(2,1)}, f32[1024,1536]{1,0:T(8,128)}, f32[1,1536]{1,0:T(1,128)}) custom-call(s32[11]{0:T(128)} %stack.59.sc_ref, bf16[2048,1024]{1,0:T(8,128)(2,1)} %get-tuple-element.35.refs_0_, ...), custom_call_target="tpu_custom_call", output_to_operand_aliasing={{0}: (16, {}), {1}: (17, {})} | custom-call | flops 14817637376 | bytes 44630016 | tf_op jit(solution)/shard_map/dw_phase/pallas_call | solution.py:340
  321.7 0.4 collective-permute-start.12
  322.1 1.3 reduce_sum.29
  324.1 0.1 pad.10.clone
  324.2 3.5 multiply_reduce_fusion
  327.7 0.1 collective-permute-start.1
  327.8 4.4 %collective-permute-done.1 = f32[3,1024]{1,0:T(4,128)S(1)} collective-permute-done((f32[3,1024]{1,0:T(4,128)S(1)}, f32[3,1024]{1,0:T(4,128)S(1)}, u32[]{:S(2)}, u32[]{:S(2)}) %collective-permute-start.1) | collective-permute-done | bytes 12320 | tf_op jit(solution)/shard_map/ppermute | solution.py:421
  332.3 0.1 fusion
  332.3 1.5 collective-permute-start.2
  333.8 2.2 collective-permute-done.2
  336.1 0.1 fusion.2
  336.2 1.5 collective-permute-start.3
  337.7 2.2 collective-permute-done.3
  340.0 0.6 fusion.1
  340.6 0.5 slice.12
  341.2 0.6 maximum_select_fusion
  341.9 12.8 %place.2.full_in = f32[1024,11264]{1,0:T(8,128)} custom-call(s32[11]{0:T(128)} %stack.59.sc_ref, f32[1024,11264]{1,0:T(8,128)} %get-tuple-element.39.full_in, f32[1024,4096]{1,0:T(8,128)} %collective-permute-done.11.refs_0_), custom_call_target="tpu_custom_call", output_to_operand_aliasing={{}: (1, {})} | custom-call | flops 5976000000 | bytes 33554432 | tf_op jit(solution)/shard_map/place/pallas_call | solution.py:396
  354.7 6.4 %place.3 = f32[1024,11264]{1,0:T(8,128)} custom-call(s32[11]{0:T(128)} %stack.59.sc_ref, f32[1024,11264]{1,0:T(8,128)} %place.2.full_in, f32[1024,1536]{1,0:T(8,128)} %collective-permute-done.12.refs_0_), custom_call_target="tpu_custom_call", output_to_operand_aliasing={{}: (1, {})} | custom-call | flops 5976000000 | bytes 12582912 | tf_op jit(solution)/shard_map/place/pallas_call | solution.py:396
  (24 shorter events, 0.3 us)
Async XLA Ops:
  38.2 39.5 %copy-start.2 = (f32[512,1024]{1,0:T(8,128)S(1)}, f32[512,1024]{1,0:T(8,128)}, u32[]{:S(2)}) copy-start(f32[512,1024]{1,0:T(8,128)} %get-tuple-element.29.p_ref.refs_0_) | copy-start | bytes 6291460
  77.7 49.6 %collective-permute-start.8 = (f32[512,1024]{1,0:T(8,128)S(1)}, f32[512,1024]{1,0:T(8,128)}, u32[]{:S(2)}, u32[]{:S(2)}) collective-permute-start(f32[512,1024]{1,0:T(8,128)S(1)} %copy-done.2), channel_id=1, source_target_pairs={{0,6},{1,7},{2,4},{3,5},{4,2},{5,3},{6,0},{7,1},{8,14},{9,15},{10,... | collective-permute-start | bytes 6291464 | tf_op jit(solution)/shard_map/ppermute | solution.py:421
  80.2 90.0 %collective-permute-start.6 = (f32[512,1024]{1,0:T(8,128)S(1)}, f32[512,1024]{1,0:T(8,128)}, u32[]{:S(2)}, u32[]{:S(2)}) collective-permute-start(f32[512,1024]{1,0:T(8,128)S(1)} %copy-done.2), channel_id=1, source_target_pairs={{0,4},{1,5},{2,6},{3,7},{4,0},{5,1},{6,2},{7,3},{8,12},{9,13},{10,... | collective-permute-start | bytes 6291464 | tf_op jit(solution)/shard_map/ppermute | solution.py:421
  80.7 89.6 %collective-permute-start.4 = (f32[512,1024]{1,0:T(8,128)S(1)}, f32[512,1024]{1,0:T(8,128)}, u32[]{:S(2)}, u32[]{:S(2)}) collective-permute-start(f32[512,1024]{1,0:T(8,128)S(1)} %copy-done.2), channel_id=1, source_target_pairs={{0,2},{1,3},{2,0},{3,1},{4,6},{5,7},{6,4},{7,5},{8,10},{9,11},{10,... | collective-permute-start | bytes 6291464 | tf_op jit(solution)/shard_map/ppermute | solution.py:421
  81.3 89.5 %collective-permute-start.10 = (f32[512,1024]{1,0:T(8,128)S(1)}, f32[512,1024]{1,0:T(8,128)}, u32[]{:S(2)}, u32[]{:S(2)}) collective-permute-start(f32[512,1024]{1,0:T(8,128)S(1)} %copy-done.2), channel_id=1, source_target_pairs={{0,1},{1,0},{2,3},{3,2},{4,5},{5,4},{6,7},{7,6},{8,9},{9,8},{10,11... | collective-permute-start | bytes 6291464 | tf_op jit(solution)/shard_map/ppermute | solution.py:421
  81.3 147.7 %collective-permute-start = (f32[512,1024]{1,0:T(8,128)}, f32[512,1024]{1,0:T(8,128)}, u32[]{:S(2)}, u32[]{:S(2)}) collective-permute-start(f32[512,1024]{1,0:T(8,128)} %get-tuple-element.26.refs_13_.refs_10_), channel_id=1, source_target_pairs={{0,8},{8,0},{1,9},{9,1},{2,10},{10,2},{3,11},{11,3},{4,12},{12,4},... | collective-permute-start | bytes 6291464 | tf_op jit(solution)/shard_map/ppermute | solution.py:440
  127.3 101.7 %collective-permute-start.9 = (f32[512,1024]{1,0:T(8,128)}, f32[512,1024]{1,0:T(8,128)}, u32[]{:S(2)}, u32[]{:S(2)}) collective-permute-start(f32[512,1024]{1,0:T(8,128)} %collective-permute-done.8.refs_2_), channel_id=1, source_target_pairs={{0,1},{1,0},{2,3},{3,2},{4,5},{5,4},{6,7},{7,6},{8,9},{9,8},{10,11... | collective-permute-start | bytes 6291464 | tf_op jit(solution)/shard_map/ppermute | solution.py:421
  170.2 58.8 %collective-permute-start.7 = (f32[512,1024]{1,0:T(8,128)}, f32[512,1024]{1,0:T(8,128)}, u32[]{:S(2)}, u32[]{:S(2)}) collective-permute-start(f32[512,1024]{1,0:T(8,128)} %collective-permute-done.6.refs_3_), channel_id=1, source_target_pairs={{0,1},{1,0},{2,3},{3,2},{4,5},{5,4},{6,7},{7,6},{8,9},{9,8},{10,11... | collective-permute-start | bytes 6291464 | tf_op jit(solution)/shard_map/ppermute | solution.py:421
  170.3 58.7 %collective-permute-start.5 = (f32[512,1024]{1,0:T(8,128)}, f32[512,1024]{1,0:T(8,128)}, u32[]{:S(2)}, u32[]{:S(2)}) collective-permute-start(f32[512,1024]{1,0:T(8,128)} %collective-permute-done.4.refs_2_), channel_id=1, source_target_pairs={{0,1},{1,0},{2,3},{3,2},{4,5},{5,4},{6,7},{7,6},{8,9},{9,8},{10,11... | collective-permute-start | bytes 6291464 | tf_op jit(solution)/shard_map/ppermute | solution.py:421
  293.1 48.8 %collective-permute-start.11 = (f32[1024,4096]{1,0:T(8,128)}, f32[1024,4096]{1,0:T(8,128)}, u32[]{:S(2)}, u32[]{:S(2)}) collective-permute-start(f32[1024,4096]{1,0:T(8,128)} %get-tuple-element.40), channel_id=1, source_target_pairs={{0,1},{1,0},{2,3},{3,2},{4,5},{5,4},{6,7},{7,6},{8,9},{9,8},{10,11... | collective-permute-start | bytes 50331656 | tf_op jit(solution)/shard_map/ppermute | solution.py:421
  321.7 33.0 %collective-permute-start.12 = (f32[1024,1536]{1,0:T(8,128)}, f32[1024,1536]{1,0:T(8,128)}, u32[]{:S(2)}, u32[]{:S(2)}) collective-permute-start(f32[1024,1536]{1,0:T(8,128)} %get-tuple-element.41), channel_id=1, source_target_pairs={{0,1},{1,0},{2,3},{3,2},{4,5},{5,4},{6,7},{7,6},{8,9},{9,8},{10,11... | collective-permute-start | bytes 18874376 | tf_op jit(solution)/shard_map/ppermute | solution.py:421
  324.2 15.8 %copy-start = (f32[1,4096]{1,0:T(1,128)S(1)}, f32[1,4096]{1,0:T(1,128)}, u32[]{:S(2)}) copy-start(f32[1,4096]{1,0:T(1,128)} %get-tuple-element.42) | copy-start | bytes 49156
  324.2 15.8 %copy-start.1 = (f32[1,1536]{1,0:T(1,128)S(1)}, f32[1,1536]{1,0:T(1,128)}, u32[]{:S(2)}) copy-start(f32[1,1536]{1,0:T(1,128)} %get-tuple-element.43) | copy-start | bytes 18436
  327.7 4.5 %collective-permute-start.1 = (f32[3,1024]{1,0:T(4,128)S(1)}, f32[3,1024]{1,0:T(4,128)S(1)}, u32[]{:S(2)}, u32[]{:S(2)}) collective-permute-start(f32[3,1024]{1,0:T(4,128)S(1)} %maximum_maximum_fusion), channel_id=1, source_target_pairs={{0,1},{1,0},{2,3},{3,2},{4,5},{5,4},{6,7},{7,6},{8,9},{9,8},{10,11... | collective-permute-start | bytes 36872 | tf_op jit(solution)/shard_map/ppermute | solution.py:421
  332.3 3.7 %collective-permute-start.2 = (f32[3,1024]{1,0:T(4,128)S(1)}, f32[3,1024]{1,0:T(4,128)S(1)}, u32[]{:S(2)}, u32[]{:S(2)}) collective-permute-start(f32[3,1024]{1,0:T(4,128)S(1)} %fusion), channel_id=1, source_target_pairs={{0,2},{1,3},{2,0},{3,1},{4,6},{5,7},{6,4},{7,5},{8,10},{9,11},{10,... | collective-permute-start | bytes 36872 | tf_op jit(solution)/shard_map/ppermute | solution.py:421
  336.2 3.7 %collective-permute-start.3 = (f32[3,1024]{1,0:T(4,128)S(1)}, f32[3,1024]{1,0:T(4,128)S(1)}, u32[]{:S(2)}, u32[]{:S(2)}) collective-permute-start(f32[3,1024]{1,0:T(4,128)S(1)} %fusion.2), channel_id=1, source_target_pairs={{0,4},{1,5},{2,6},{3,7},{4,0},{5,1},{6,2},{7,3},{8,12},{9,13},{10,... | collective-permute-start | bytes 36872 | tf_op jit(solution)/shard_map/ppermute | solution.py:421
  340.0 1.2 collective-permute-start.13
